TPU v7x, 256 devices: a whole 4x4x8 slice. The times are simulated.
256 devices in a mesh: trial: 2 (over core), bank: 4 (over x), zero: 32 (over z, y).
Axes of the slice: x: 4, y: 4, z: 8, core: 2. Of those that a mesh axis runs over, the one named last changes fastest.
Arguments:
- w_gate: float32 [128, 2048, 1024], P(('trial', 'bank'), 'zero'), parts along dimension 0, may hold values from -0.25 to 0.25
- w_up: float32 [128, 2048, 1024], P(('trial', 'bank'), 'zero'), parts along dimension 0, may hold values from -0.25 to 0.25
- router_weight: float32 [4096, 64], P(('trial', 'zero'), 'bank'), parts along dimension 0, may hold values from -0.125 to 0.125
- router_gain: float32 [4096], P(('trial', 'zero')), parts along dimension 0, may hold values from 0.25 to 1.75
Outputs:
- serve_gate: bfloat16 [128, 2048, 1024], P(('trial', 'bank'), None, 'zero'), parts along dimension 0
- serve_up: bfloat16 [128, 2048, 1024], P(('trial', 'bank'), None, 'zero'), parts along dimension 0
- scale_gate: float32 [128, 1024], P(('trial', 'bank'), 'zero'), parts along dimension 0
- scale_up: float32 [128, 1024], P(('trial', 'bank'), 'zero'), parts along dimension 0
- serve_router: bfloat16 [4096, 64], P('trial'), parts along dimension 0
There are 2 independent parts, one for each index of `trial`. A program takes and returns all parts, laid end to end along the dimension named above; each array names one. Nothing has to cross between parts.
All inputs are finite; a program needn't handle non-finite values. Where the computation divides by a largest or mean magnitude, that divisor is 1e-20 or more.
Results may differ from a plain program's by a relative error of at most 0.001.
Values may be sent and summed in bfloat16 or wider, within the bound.
No kernel may reach another device: no remote copies, remote signals or barrier semaphores. Data moves between devices by JAX's collectives and lax.ppermute only.
A program may use at most 128 MiB of HBM per device.

v0:
```python
import jax
import jax.numpy as jnp
from jax import lax
from jax.sharding import PartitionSpec as P

D_MODEL = 2048


def rows_for(lines, count):
    spare = -lines.shape[0] % count
    if not spare:
        return lines
    return jnp.concatenate([lines, jnp.zeros((spare, *lines.shape[1:]), lines.dtype)])


def sent_to_all(array, axis):
    count = lax.axis_size(axis)
    return lax.all_to_all(
        jnp.broadcast_to(array[None], (count, *array.shape)), axis, 0, 0, tiled=True
    )


def laid_out(tiles, dim):
    dims = list(tiles.shape[1:])
    dims[dim] *= tiles.shape[0]
    return jnp.moveaxis(tiles, 0, dim).reshape(dims)


def gathered_copies(array, axis, dim):
    tiles = sent_to_all(array, axis)
    return laid_out(tiles, dim)


def in_blocks(array, dim, count):
    dims = array.shape
    tiles = array.reshape(*dims[:dim], count, dims[dim] // count, *dims[dim + 1 :])
    return jnp.moveaxis(tiles, dim, 0)


def summed_on_arrival(array, axis, dim):
    tiles = in_blocks(array, dim, lax.axis_size(axis))
    arrived = lax.all_to_all(tiles, axis, split_axis=0, concat_axis=0, tiled=True)
    return arrived.sum(axis=0)


def total_of(array, axes):
    padded = rows_for(array, lax.axis_size(axes))
    whole = gathered_copies(summed_on_arrival(padded, axes, 0), axes, 0)
    return lax.slice_in_dim(whole, 0, len(array)).reshape(array.shape)


def packed_total(arrays, axis):
    ravelled, at, finished = (jnp.concatenate([a.reshape(-1) for a in arrays]), 0, [])
    total = total_of(ravelled, axis)
    for a in arrays:
        finished.append(total[at : at + a.size].reshape(a.shape))
        at += a.size
    return tuple(finished)


def local(w_gate, w_up, router_weight, router_gain):
    total_gate, total_up = packed_total(
        (jnp.sum(jnp.abs(w_gate), axis=1), jnp.sum(jnp.abs(w_up), axis=1)), "zero"
    )
    scale_gate = total_gate / D_MODEL
    scale_up = total_up / D_MODEL
    narrow_gate, narrow_up = (
        (w_gate / jnp.expand_dims(scale_gate, 1)).astype(jnp.bfloat16),
        (w_up / jnp.expand_dims(scale_up, 1)).astype(jnp.bfloat16),
    )
    serve_gate, serve_up = (
        lax.all_to_all(narrow_gate, "zero", split_axis=2, concat_axis=1, tiled=True),
        lax.all_to_all(narrow_up, "zero", split_axis=2, concat_axis=1, tiled=True),
    )
    scale_gate = lax.dynamic_slice_in_dim(
        scale_gate, lax.axis_index("zero") * serve_gate.shape[2], serve_gate.shape[2], axis=1
    )
    scale_up = lax.dynamic_slice_in_dim(
        scale_up, lax.axis_index("zero") * serve_up.shape[2], serve_up.shape[2], axis=1
    )
    part_router = (router_weight * router_gain[:, None]).astype(jnp.bfloat16)
    row_router = gathered_copies(part_router, "zero", 0)
    serve_router = gathered_copies(row_router, "bank", 1)
    return (serve_gate, serve_up, scale_gate, scale_up, serve_router)


def solution(mesh):
    placed = (
        P(("trial", "bank"), "zero", None),
        P(("trial", "bank"), "zero", None),
        P(("trial", "zero"), "bank"),
        P(("trial", "zero")),
    )
    return jax.shard_map(
        local,
        mesh=mesh,
        in_specs=placed,
        out_specs=(
            P(("trial", "bank"), None, "zero"),
            P(("trial", "bank"), None, "zero"),
            P(("trial", "bank"), "zero"),
            P(("trial", "bank"), "zero"),
            P("trial", None),
        ),
        check_vma=False,
    )
```

profile of v0, /device:TPU:10, one launch (start us, length us, event | category | flops | bytes accessed | tf_op | source)
XLA Modules:
  0.0 207.8 jit_solution(914936306891506960)
XLA Ops:
  0.7 5.0 %abs_reduce_fusion = (f32[16,1024]{1,0:T(8,128)S(1)}, f32[16,1024]{1,0:T(8,128)S(1)}) fusion(f32[16,64,1024]{2,1,0:T(8,128)} %param.5, f32[16,64,1024]{2,1,0:T(8,128)} %param.4), kind=kLoop, calls=%fused_computation.2 | loop fusion | flops 4161536 | bytes 8519680 | tf_op jit(solution)/shard_map/reduce_sum | solution.py:63
  5.7 0.7 all_to_all.42
  6.5 11.7 %all-to-all-start = ((f32[32,1,1024]{2,1,0:T(1,128)}), f32[32,1,1024]{2,1,0:T(1,128)S(1)}, u32[]{:S(2)}, u32[]{:S(2)}) async-start(f32[32,1,1024]{2,1,0:T(1,128)} %all_to_all.42), calls=%async_computation | async-start | bytes 262144 | tf_op jit(solution)/shard_map/all_to_all | solution.py:42
  18.2 0.8 reshape.53
  19.0 8.0 %all-to-all-done = f32[32,1,1024]{2,1,0:T(1,128)S(1)} async-done(((f32[32,1,1024]{2,1,0:T(1,128)}), f32[32,1,1024]{2,1,0:T(1,128)S(1)}, u32[]{:S(2)}, u32[]{:S(2)}) %all-to-all-start) | async-done | bytes 131104 | tf_op jit(solution)/shard_map/all_to_all | solution.py:42
  27.0 5.3 %all-to-all-start.4 = ((bf16[32,2,512]{2,1,0:T(2,128)(2,1)}), bf16[32,2,512]{2,1,0:T(2,128)(2,1)S(1)}, u32[]{:S(2)}, u32[]{:S(2)}) async-start(bf16[32,2,512]{2,1,0:T(2,128)(2,1)} %reshape.53), calls=%async_computation.4 | async-start | bytes 131072 | tf_op jit(solution)/shard_map/all_to_all | solution.py:18
  32.5 8.6 %all-to-all-done.4 = bf16[32,2,512]{2,1,0:T(2,128)(2,1)S(1)} async-done(((bf16[32,2,512]{2,1,0:T(2,128)(2,1)}), bf16[32,2,512]{2,1,0:T(2,128)(2,1)S(1)}, u32[]{:S(2)}, u32[]{:S(2)}) %all-to-all-start.4) | async-done | bytes 65568 | tf_op jit(solution)/shard_map/all_to_all | solution.py:18
  41.1 0.7 broadcast_in_dim.8
  41.8 5.2 %all-to-all-start.1 = ((f32[32,1,1024]{2,1,0:T(1,128)}), f32[32,1,1024]{2,1,0:T(1,128)S(1)}, u32[]{:S(2)}, u32[]{:S(2)}) async-start(f32[32,1,1024]{2,1,0:T(1,128)} %broadcast_in_dim.8), calls=%async_computation.1 | async-start | bytes 262144 | tf_op jit(solution)/shard_map/all_to_all | solution.py:18
  47.0 8.1 %copy.30 = f32[16,64,1024]{1,0,2:T(8,128)} copy(f32[16,64,1024]{2,1,0:T(8,128)} %param.5) | data formatting | bytes 8388608 | tf_op args[1]
  55.5 0.5 all-to-all-done.1
  56.0 0.7 broadcast_in_dim.11
  56.7 4.8 %all-to-all-start.5 = ((bf16[4,2048,16]{1,2,0:T(8,128)(2,1)}), bf16[4,2048,16]{1,2,0:T(8,128)(2,1)S(1)}, u32[]{:S(2)}, u32[]{:S(2)}) async-start(bf16[4,2048,16]{1,2,0:T(8,128)(2,1)} %broadcast_in_dim.11), calls=%async_computation.5 | async-start | bytes 524288 | tf_op jit(solution)/shard_map/all_to_all | solution.py:18
  61.7 0.2 copy.36
  61.9 6.9 %fusion.1 = bf16[1024,16,64]{2,1,0:T(8,128)(2,1)} fusion(f32[16,64,1024]{1,0,2:T(8,128)} %copy.30, f32[16,1024]{0,1:T(8,128)S(1)} %bitcast.34), kind=kLoop, calls=%fused_computation.11 | loop fusion | flops 2097152 | bytes 6356992
  68.8 7.9 %reshape.51 = bf16[32,2,16384]{2,1,0:T(2,128)(2,1)} reshape(bf16[1024,16,64]{2,1,0:T(8,128)(2,1)} %fusion.1) | data formatting | bytes 4194304
  76.6 9.4 %all-to-all-start.3 = ((bf16[32,2,16384]{2,1,0:T(2,128)(2,1)}), bf16[32,2,16384]{2,1,0:T(2,128)(2,1)S(1)}, u32[]{:S(2)}, u32[]{:S(2)}) async-start(bf16[32,2,16384]{2,1,0:T(2,128)(2,1)} %reshape.51), calls=%async_computation.3 | async-start | bytes 4194304 | tf_op jit(solution)/shard_map/all_to_all | solution.py:73
  86.0 8.1 %copy.26 = f32[16,64,1024]{1,0,2:T(8,128)} copy(f32[16,64,1024]{2,1,0:T(8,128)} %param.4) | data formatting | bytes 8388608 | tf_op args[0]
  94.3 6.9 %fusion = bf16[1024,16,64]{2,1,0:T(8,128)(2,1)} fusion(f32[16,64,1024]{1,0,2:T(8,128)} %copy.26, f32[16,1024]{0,1:T(8,128)S(1)} %bitcast.35), kind=kLoop, calls=%fused_computation.10 | loop fusion | flops 2097152 | bytes 6356992
  101.2 7.9 %reshape.49 = bf16[32,2,16384]{2,1,0:T(2,128)(2,1)} reshape(bf16[1024,16,64]{2,1,0:T(8,128)(2,1)} %fusion) | data formatting | bytes 4194304
  109.1 24.1 %all-to-all-done.3 = bf16[32,2,16384]{2,1,0:T(2,128)(2,1)S(1)} async-done(((bf16[32,2,16384]{2,1,0:T(2,128)(2,1)}), bf16[32,2,16384]{2,1,0:T(2,128)(2,1)S(1)}, u32[]{:S(2)}, u32[]{:S(2)}) %all-to-all-start.3) | async-done | bytes 2097184 | tf_op jit(solution)/shard_map/all_to_all | solution.py:73
  133.2 5.6 %all-to-all-start.2 = ((bf16[32,2,16384]{2,1,0:T(2,128)(2,1)}), bf16[32,2,16384]{2,1,0:T(2,128)(2,1)}, u32[]{:S(2)}, u32[]{:S(2)}) async-start(bf16[32,2,16384]{2,1,0:T(2,128)(2,1)} %reshape.49), calls=%async_computation.2 | async-start | bytes 4194304 | tf_op jit(solution)/shard_map/all_to_all | solution.py:72
  138.8 0.7 constant_dynamic-slice_fusion.1
  139.5 0.7 constant_dynamic-slice_fusion
  140.2 4.0 %reshape.52 = bf16[1024,16,64]{2,1,0:T(8,128)(2,1)} reshape(bf16[32,2,16384]{2,1,0:T(2,128)(2,1)S(1)} %all-to-all-done.3) | data formatting | bytes 4194304
  144.2 6.9 %copy.32 = bf16[16,32,64,32]{2,1,3,0:T(8,128)(2,1)} copy(bf16[16,32,64,32]{2,0,3,1:T(8,128)(2,1)} %bitcast.32) | data formatting | bytes 4194304 | tf_op jit(solution)/shard_map/all_to_all | solution.py:73
  151.1 6.7 %all_to_all.52 = bf16[16,2048,32]{1,2,0:T(8,128)(2,1)} reshape(bf16[16,32,64,32]{2,1,3,0:T(8,128)(2,1)} %copy.32) | data formatting | bytes 4194304 | tf_op jit(solution)/shard_map/all_to_all | solution.py:73
  157.8 27.8 %all-to-all-done.2 = bf16[32,2,16384]{2,1,0:T(2,128)(2,1)} async-done(((bf16[32,2,16384]{2,1,0:T(2,128)(2,1)}), bf16[32,2,16384]{2,1,0:T(2,128)(2,1)}, u32[]{:S(2)}, u32[]{:S(2)}) %all-to-all-start.2) | async-done | bytes 2097184 | tf_op jit(solution)/shard_map/all_to_all | solution.py:72
  185.6 7.9 %reshape.50 = bf16[1024,16,64]{2,1,0:T(8,128)(2,1)} reshape(bf16[32,2,16384]{2,1,0:T(2,128)(2,1)} %all-to-all-done.2) | data formatting | bytes 4194304
  193.5 6.9 %copy.28 = bf16[16,32,64,32]{2,1,3,0:T(8,128)(2,1)} copy(bf16[16,32,64,32]{2,0,3,1:T(8,128)(2,1)} %bitcast.33) | data formatting | bytes 4194304 | tf_op jit(solution)/shard_map/all_to_all | solution.py:72
  200.4 6.7 %all_to_all.48 = bf16[16,2048,32]{1,2,0:T(8,128)(2,1)} reshape(bf16[16,32,64,32]{2,1,3,0:T(8,128)(2,1)} %copy.28) | data formatting | bytes 4194304 | tf_op jit(solution)/shard_map/all_to_all | solution.py:72
  207.1 0.7 copy.39
  (14 shorter events, 0.8 us)
Async XLA Ops:
  0.6 17.5 %copy-start = (f32[64,16]{0,1:T(8,128)S(1)}, f32[64,16]{0,1:T(8,128)}, u32[]{:S(2)}) copy-start(f32[64,16]{0,1:T(8,128)} %param.6) | copy-start | bytes 12292
  0.6 17.5 %copy-start.1 = (f32[64]{0:T(128)S(1)}, f32[64]{0:T(128)}, u32[]{:S(2)}) copy-start(f32[64]{0:T(128)} %param.7) | copy-start | bytes 772
  6.5 20.6 %all-to-all-start = ((f32[32,1,1024]{2,1,0:T(1,128)}), f32[32,1,1024]{2,1,0:T(1,128)S(1)}, u32[]{:S(2)}, u32[]{:S(2)}) async-start(f32[32,1,1024]{2,1,0:T(1,128)} %all_to_all.42), calls=%async_computation | async-start | bytes 262144 | tf_op jit(solution)/shard_map/all_to_all | solution.py:42
  27.0 14.1 %all-to-all-start.4 = ((bf16[32,2,512]{2,1,0:T(2,128)(2,1)}), bf16[32,2,512]{2,1,0:T(2,128)(2,1)S(1)}, u32[]{:S(2)}, u32[]{:S(2)}) async-start(bf16[32,2,512]{2,1,0:T(2,128)(2,1)} %reshape.53), calls=%async_computation.4 | async-start | bytes 131072 | tf_op jit(solution)/shard_map/all_to_all | solution.py:18
  41.8 14.2 %all-to-all-start.1 = ((f32[32,1,1024]{2,1,0:T(1,128)}), f32[32,1,1024]{2,1,0:T(1,128)S(1)}, u32[]{:S(2)}, u32[]{:S(2)}) async-start(f32[32,1,1024]{2,1,0:T(1,128)} %broadcast_in_dim.8), calls=%async_computation.1 | async-start | bytes 262144 | tf_op jit(solution)/shard_map/all_to_all | solution.py:18
  56.7 19.9 %all-to-all-start.5 = ((bf16[4,2048,16]{1,2,0:T(8,128)(2,1)}), bf16[4,2048,16]{1,2,0:T(8,128)(2,1)S(1)}, u32[]{:S(2)}, u32[]{:S(2)}) async-start(bf16[4,2048,16]{1,2,0:T(8,128)(2,1)} %broadcast_in_dim.11), calls=%async_computation.5 | async-start | bytes 524288 | tf_op jit(solution)/shard_map/all_to_all | solution.py:18
  76.6 56.5 %all-to-all-start.3 = ((bf16[32,2,16384]{2,1,0:T(2,128)(2,1)}), bf16[32,2,16384]{2,1,0:T(2,128)(2,1)S(1)}, u32[]{:S(2)}, u32[]{:S(2)}) async-start(bf16[32,2,16384]{2,1,0:T(2,128)(2,1)} %reshape.51), calls=%async_computation.3 | async-start | bytes 4194304 | tf_op jit(solution)/shard_map/all_to_all | solution.py:73
  133.2 52.4 %all-to-all-start.2 = ((bf16[32,2,16384]{2,1,0:T(2,128)(2,1)}), bf16[32,2,16384]{2,1,0:T(2,128)(2,1)}, u32[]{:S(2)}, u32[]{:S(2)}) async-start(bf16[32,2,16384]{2,1,0:T(2,128)(2,1)} %reshape.49), calls=%async_computation.2 | async-start | bytes 4194304 | tf_op jit(solution)/shard_map/all_to_all | solution.py:72
where the time goes:
time: 209 us; the launch traced here: 208 us
  local copies, waits for them, and re-layouts  76.9 us (37%)
  waiting for transfers between devices  69.1 us (33%)
  starting transfers between devices  42 us (20%)
  other arithmetic  19 us (9%)
    unnamed x14, local copies, waits for them, and re-layouts  45.5 us
    all_to_all x1, waiting for transfers between devices, local(): lax.all_to_all(narrow_gate, 'zero', split_axis=2, concat_axis=1, tiled=True)  27.8 us
    all_to_all x1, waiting for transfers between devices, local(): lax.all_to_all(narrow_up, 'zero', split_axis=2, concat_axis=1, tiled=True)  24.1 us
    all_to_all x3, starting transfers between devices, sent_to_all(): lax.all_to_all(jnp.broadcast_to(array[None], (count, *array.shape)), axis...  15.3 us
    unnamed x2, other arithmetic  13.8 us
    all_to_all x2, local copies, waits for them, and re-layouts, local(): lax.all_to_all(narrow_up, 'zero', split_axis=2, concat_axis=1, tiled=True)  13.6 us
    all_to_all x2, local copies, waits for them, and re-layouts, local(): lax.all_to_all(narrow_gate, 'zero', split_axis=2, concat_axis=1, tiled=True)  13.6 us
    all_to_all x1, starting transfers between devices, summed_on_arrival(): lax.all_to_all(tiles, axis, split_axis=0, concat_axis=0, tiled=True)  11.7 us
  transfers between devices with their start and end apart: 6, of which 5 were waited for; matrix products, arithmetic and copies ran while one was open for 29% of the time, Pallas kernels for 0%

commit v1 on v0

v1 whole, which is shorter than its diff:
```python
import jax
import jax.numpy as jnp
from jax import lax
from jax.experimental import pallas as pl
from jax.experimental.pallas import tpu as pltpu
from jax.sharding import PartitionSpec as P

D_MODEL = 2048
LANES = 128
SPAN = 250.0
LN2 = 0.6931471805599453


def coded(w):
    size = jnp.abs(w)
    total = jnp.sum(size, axis=0, keepdims=True)
    top = jnp.max(size, axis=0, keepdims=True)
    top = (top * (1 + 2.0**-7)).astype(jnp.bfloat16).astype(jnp.float32)
    per = jnp.where(top > 1e-30, SPAN / jnp.maximum(top, 1e-30), 0.0)
    code = jnp.exp2(size * per - SPAN / 2)
    high = total.astype(jnp.bfloat16).astype(jnp.float32)
    return jnp.where(w < 0, -code, code), top, high, total - high


def encode_kernel(gate_ref, up_ref, out_ref, stats_ref, *, experts, bands):
    e = pl.program_id(0)

    @pl.when(e < experts)
    def _():
        gate, *gate_stats = coded(gate_ref[0])
        up, *up_stats = coded(up_ref[0])
        for k, (g, u) in enumerate(zip(gate_stats, up_stats)):
            stats_ref[pl.ds(2 * k * experts + e, 1)] = g
            stats_ref[pl.ds((2 * k + 1) * experts + e, 1)] = u
        both = jnp.concatenate([gate, up], axis=0)
        for t in range(bands):
            tile = both[:, t * LANES : (t + 1) * LANES].T.astype(jnp.bfloat16)
            for y in range(4):
                out_ref[4 * t + y] = tile[32 * y : 32 * (y + 1)]

    @pl.when(e == experts)
    def _():
        for t in range(bands):
            tile = stats_ref[:, t * LANES : (t + 1) * LANES].T.astype(jnp.bfloat16)
            for y in range(4):
                out_ref[4 * t + y] = tile[32 * y : 32 * (y + 1)]


def encode(w_gate, w_up):
    experts, rows, columns = w_gate.shape
    last = experts - 1
    return pl.pallas_call(
        lambda *refs: encode_kernel(*refs, experts=experts, bands=columns // LANES),
        name="encode",
        grid=(experts + 1,),
        in_specs=[pl.BlockSpec((1, rows, columns), lambda e: (jnp.minimum(e, last), 0, 0))] * 2,
        out_specs=pl.BlockSpec((32, 32, LANES), lambda e: (0, e, 0)),
        out_shape=jax.ShapeDtypeStruct((32, 32 * (experts + 1), LANES), jnp.bfloat16),
        scratch_shapes=[pltpu.VMEM((LANES, columns), jnp.float32)],
        compiler_params=pltpu.CompilerParams(vmem_limit_bytes=60 << 20),
    )(w_gate, w_up)


def decode_kernel(got_ref, stats_ref, gate_ref, up_ref, gate_scale_ref, up_scale_ref, factor_ref, *, experts):
    e = pl.program_id(0)

    @pl.when(e == 0)
    def _():
        stats = stats_ref[...].astype(jnp.float32)
        total = jnp.sum(stats, axis=0)
        total = pltpu.roll(total, LANES - 2 * experts, 1) + pltpu.roll(total, LANES - 4 * experts, 1)
        scale = total / D_MODEL
        factor_ref[...] = stats * (1.0 / (SPAN * LN2)) / scale[None]
        turned = jnp.concatenate([scale] * 4, axis=0).T
        gate_scale_ref[...] = turned[:experts, :32]
        up_scale_ref[...] = turned[experts : 2 * experts, :32]

    left = lax.broadcasted_iota(jnp.int32, (32, LANES), 1) < 64

    def value(s):
        code = got_ref[s].astype(jnp.float32)
        factor = pltpu.roll(factor_ref[s], LANES - e, 1)
        factor = jnp.where(left, factor[:, :1], factor[:, experts : experts + 1])
        size = (jnp.log(jnp.abs(code)) + SPAN / 2 * LN2) * factor
        return jnp.where(code < 0, -size, size)

    for p in range(16):
        one, two = value(2 * p), value(2 * p + 1)
        gate_ref[0, :, p * LANES : (p + 1) * LANES] = jnp.where(left, one, pltpu.roll(two, 64, 1)).astype(jnp.bfloat16)
        up_ref[0, :, p * LANES : (p + 1) * LANES] = jnp.where(left, pltpu.roll(one, 64, 1), two).astype(jnp.bfloat16)


def decode(got, experts):
    out = jax.ShapeDtypeStruct((experts, 32, D_MODEL), jnp.bfloat16)
    scale = jax.ShapeDtypeStruct((experts, 32), jnp.float32)
    return pl.pallas_call(
        lambda *refs: decode_kernel(*refs, experts=experts),
        name="decode",
        grid=(experts,),
        in_specs=[
            pl.BlockSpec((32, 32, LANES), lambda e: (0, e, 0)),
            pl.BlockSpec((32, 32, LANES), lambda e: (0, experts, 0)),
        ],
        out_specs=[pl.BlockSpec((1, 32, D_MODEL), lambda e: (e, 0, 0))] * 2
        + [pl.BlockSpec((experts, 32), lambda e: (0, 0))] * 2,
        out_shape=[out, out, scale, scale],
        scratch_shapes=[pltpu.VMEM((32, 32, LANES), jnp.float32)],
        compiler_params=pltpu.CompilerParams(vmem_limit_bytes=60 << 20),
    )(got, got)


def sent_to_all(array, axis):
    count = lax.axis_size(axis)
    return lax.all_to_all(jnp.broadcast_to(array[None], (count, *array.shape)), axis, 0, 0, tiled=True)


def local(w_gate, w_up, router_weight, router_gain):
    router = (router_weight * router_gain[:, None]).astype(jnp.bfloat16).T
    router = jnp.moveaxis(sent_to_all(router, "zero"), 0, 1).reshape(router.shape[0], D_MODEL)
    router = sent_to_all(router, "bank").reshape(-1, D_MODEL).T
    sent = encode(w_gate, w_up)
    got = lax.all_to_all(sent, "zero", 0, 0, tiled=True)
    gate, up, scale_gate, scale_up = decode(got, w_gate.shape[0])
    return jnp.swapaxes(gate, 1, 2), jnp.swapaxes(up, 1, 2), scale_gate, scale_up, router


def solution(mesh):
    placed = (
        P(("trial", "bank"), "zero", None),
        P(("trial", "bank"), "zero", None),
        P(("trial", "zero"), "bank"),
        P(("trial", "zero")),
    )
    return jax.shard_map(
        local,
        mesh=mesh,
        in_specs=placed,
        out_specs=(
            P(("trial", "bank"), None, "zero"),
            P(("trial", "bank"), None, "zero"),
            P(("trial", "bank"), "zero"),
            P(("trial", "bank"), "zero"),
            P("trial", None),
        ),
        check_vma=False,
    )
```

time: 209 us -> 198 us (0.947)
  local copies, waits for them, and re-layouts: 76.9 us -> 1.93 us
  Pallas kernels: 0 us -> 63.1 us
  starting transfers between devices: 42 us -> 10.8 us
  waiting for transfers between devices: 69.1 us -> 97.9 us
  blocking collectives: 0 us -> 20.2 us
  other arithmetic: 19 us -> 0.7 us
    pallas_call x0 -> x2, Pallas kernels: none -> 63.1 us  [the longest x1 49.8 us: decode(): pl.pallas_call(lambda *refs: decode_kernel(*refs, experts=experts), name=...]
    unnamed x14 -> x3, local copies, waits for them, and re-layouts: 45.5 us -> 0.98 us
    all_to_all x3 -> x1, waiting for transfers between devices: 59.9 us -> 97.9 us  [local(): got = lax.all_to_all(sent, 'zero', 0, 0, tiled=True)]
    all_to_all x6 -> x0, local copies, waits for them, and re-layouts: 28 us -> none  [the longest x2 13.6 us: local(): lax.all_to_all(narrow_up, 'zero', split_axis=2, concat_axis=1, tiled=True)]
    all_to_all x3 -> x1, starting transfers between devices: 26.7 us -> 5.96 us  [local(): got = lax.all_to_all(sent, 'zero', 0, 0, tiled=True)]
    all_to_all x0 -> x1, blocking collectives: none -> 20.2 us  [sent_to_all(): lax.all_to_all(jnp.broadcast_to(array[None], (count, *array.shape)), axis...]
    unnamed x2 -> x0, other arithmetic: 13.8 us -> none
    all_to_all x3 -> x1, starting transfers between devices: 15.3 us -> 4.82 us  [sent_to_all(): lax.all_to_all(jnp.broadcast_to(array[None], (count, *array.shape)), axis...]
  transfers between devices with their start and end apart: 6 -> 2, of which waited for: 5 -> 1; matrix products, arithmetic and copies ran while one was open for 29% -> 0% of each run, Pallas kernels for 0% -> 7%
where the time goes in v1:
time: 198 us; the launch traced here: 195 us
  waiting for transfers between devices  97.9 us (49%)
  Pallas kernels  63.1 us (32%)
  blocking collectives  20.2 us (10%)
  starting transfers between devices  10.8 us (5%)
    all_to_all x1, waiting for transfers between devices, local(): got = lax.all_to_all(sent, 'zero', 0, 0, tiled=True)  97.9 us
    pallas_call x1, Pallas kernels, decode(): pl.pallas_call(lambda *refs: decode_kernel(*refs, experts=experts), name=...  49.8 us
    all_to_all x1, blocking collectives, sent_to_all(): lax.all_to_all(jnp.broadcast_to(array[None], (count, *array.shape)), axis...  20.2 us
    pallas_call x1, Pallas kernels, encode(): pl.pallas_call(lambda *refs: encode_kernel(*refs, experts=experts, bands=...  13.3 us
    all_to_all x1, starting transfers between devices, local(): got = lax.all_to_all(sent, 'zero', 0, 0, tiled=True)  5.96 us
    all_to_all x1, starting transfers between devices, sent_to_all(): lax.all_to_all(jnp.broadcast_to(array[None], (count, *array.shape)), axis...  4.82 us
  transfers between devices with their start and end apart: 2, of which 1 were waited for; matrix products, arithmetic and copies ran while one was open for 0% of the time, Pallas kernels for 7%

profile of v1, /device:TPU:10, one launch (start us, length us, event | category | flops | bytes accessed | tf_op | source)
XLA Modules:
  0.0 195.2 jit_solution(17906111079606841303)
XLA Ops:
  0.6 0.7 fusion
  1.4 0.1 reshape.17
  1.5 20.2 %all_to_all.15 = bf16[32,2,512]{2,1,0:T(2,128)(2,1)S(1)} all-to-all(bf16[32,2,512]{2,1,0:T(2,128)(2,1)S(1)} %reshape.17), channel_id=1, replica_groups=mesh['trial'=2,'bank'=4,'zero'=32] {'zero'}, dimensions={0} | all-to-all | bytes 131072 | tf_op jit(solution)/shard_map/all_to_all | solution.py:114
  21.7 0.1 reshape.18
  21.9 0.2 broadcast_in_dim.7
  22.1 0.7 broadcast_in_dim.16
  22.8 4.8 %all-to-all-start.2 = ((bf16[4,16,2048]{2,1,0:T(8,128)(2,1)}), bf16[4,16,2048]{2,1,0:T(8,128)(2,1)S(1)}, u32[]{:S(2)}, u32[]{:S(2)}) async-start(bf16[4,16,2048]{2,1,0:T(8,128)(2,1)} %broadcast_in_dim.16), calls=%async_computation.2 | async-start | bytes 524288 | tf_op jit(solution)/shard_map/all_to_all | solution.py:114
  27.6 13.3 %encode.1 = bf16[32,544,128]{2,1,0:T(8,128)(2,1)} custom-call(f32[16,64,1024]{2,1,0:T(8,128)} %refs_0_.1, f32[16,64,1024]{2,1,0:T(8,128)} %refs_1_.1), custom_call_target="tpu_custom_call" | custom-call | tf_op jit(solution)/shard_map/encode/pallas_call | solution.py:52
  40.9 0.0 all-to-all-done.2
  40.9 6.0 %all-to-all-start = ((bf16[32,544,128]{2,1,0:T(8,128)(2,1)}), bf16[32,544,128]{2,1,0:T(8,128)(2,1)}, u32[]{:S(2)}, u32[]{:S(2)}) async-start(bf16[32,544,128]{2,1,0:T(8,128)(2,1)} %encode.1), calls=%async_computation | async-start | bytes 8912896 | tf_op jit(solution)/shard_map/all_to_all | solution.py:122
  46.9 97.9 %all-to-all-done.refs_0_.refs_1_ = bf16[32,544,128]{2,1,0:T(8,128)(2,1)} async-done(((bf16[32,544,128]{2,1,0:T(8,128)(2,1)}), bf16[32,544,128]{2,1,0:T(8,128)(2,1)}, u32[]{:S(2)}, u32[]{:S(2)}) %all-to-all-start) | async-done | bytes 4456480 | tf_op jit(solution)/shard_map/all_to_all | solution.py:122
  144.7 49.8 %decode.1 = (bf16[16,32,2048]{2,1,0:T(8,128)(2,1)}, bf16[16,32,2048]{2,1,0:T(8,128)(2,1)}, f32[16,32]{1,0:T(8,128)}, f32[16,32]{1,0:T(8,128)}) custom-call(bf16[32,544,128]{2,1,0:T(8,128)(2,1)} %all-to-all-done.refs_0_.refs_1_, bf16[32,544,128]{2,1,0:T(8,128)(2,1)} %all-to-all-done.refs_0_.refs_1_), custom_call_target="tpu_custom_call" | custom-call | tf_op jit(solution)/shard_map/decode/pallas_call | solution.py:96
  194.5 0.7 copy.11
  (2 shorter events, 0.1 us)
Async XLA Ops:
  22.8 18.1 %all-to-all-start.2 = ((bf16[4,16,2048]{2,1,0:T(8,128)(2,1)}), bf16[4,16,2048]{2,1,0:T(8,128)(2,1)S(1)}, u32[]{:S(2)}, u32[]{:S(2)}) async-start(bf16[4,16,2048]{2,1,0:T(8,128)(2,1)} %broadcast_in_dim.16), calls=%async_computation.2 | async-start | bytes 524288 | tf_op jit(solution)/shard_map/all_to_all | solution.py:114
  40.9 103.8 %all-to-all-start = ((bf16[32,544,128]{2,1,0:T(8,128)(2,1)}), bf16[32,544,128]{2,1,0:T(8,128)(2,1)}, u32[]{:S(2)}, u32[]{:S(2)}) async-start(bf16[32,544,128]{2,1,0:T(8,128)(2,1)} %encode.1), calls=%async_computation | async-start | bytes 8912896 | tf_op jit(solution)/shard_map/all_to_all | solution.py:122

commit v2 on v1

v2 whole, which is shorter than its diff:
```python
import jax
import jax.numpy as jnp
from jax import lax
from jax.experimental import pallas as pl
from jax.experimental.pallas import tpu as pltpu
from jax.sharding import PartitionSpec as P

D_MODEL = 2048
LANES = 128
SPAN = 250.0
LN2 = 0.6931471805599453


def coded(w):
    size = jnp.abs(w)
    total = jnp.sum(size, axis=0, keepdims=True)
    top = jnp.max(size, axis=0, keepdims=True)
    top = (top * (1 + 2.0**-7)).astype(jnp.bfloat16).astype(jnp.float32)
    per = jnp.where(top > 1e-30, SPAN / jnp.maximum(top, 1e-30), 0.0)
    code = jnp.exp2(size * per - SPAN / 2)
    high = total.astype(jnp.bfloat16).astype(jnp.float32)
    return jnp.where(w < 0, -code, code), top, high, total - high


def encode_kernel(gate_ref, up_ref, out_ref, stats_ref, *, experts, bands, group):
    step = pl.program_id(0)

    @pl.when(step < experts // group)
    def _():
        def one(i, _):
            e = step * group + i
            row = pl.multiple_of(i * 32, 32)
            kept = []
            for t in range(bands):
                lanes = slice(t * LANES, (t + 1) * LANES)
                gate, *gate_stats = coded(gate_ref[i, :, lanes])
                up, *up_stats = coded(up_ref[i, :, lanes])
                kept.append([v for pair in zip(gate_stats, up_stats) for v in pair])
                tile = jnp.concatenate([gate, up], axis=0).T.astype(jnp.bfloat16)
                for y in range(4):
                    out_ref[4 * t + y, pl.ds(row, 32)] = tile[32 * y : 32 * (y + 1)]
            for k, parts in enumerate(zip(*kept)):
                stats_ref[pl.ds(k * experts + e, 1)] = jnp.concatenate(parts, axis=1)

        lax.fori_loop(0, group, one, None, unroll=UNROLL)

    @pl.when(step == experts // group)
    def _():
        for t in range(bands):
            tile = stats_ref[:, t * LANES : (t + 1) * LANES].T.astype(jnp.bfloat16)
            for y in range(4):
                out_ref[4 * t + y, :32] = tile[32 * y : 32 * (y + 1)]


GROUP = 4
UNROLL = 2


def encode(w_gate, w_up):
    experts, rows, columns = w_gate.shape
    group = GROUP
    last = experts // group - 1
    return pl.pallas_call(
        lambda *refs: encode_kernel(*refs, experts=experts, bands=columns // LANES, group=group),
        name="encode",
        grid=(experts // group + 1,),
        in_specs=[pl.BlockSpec((group, rows, columns), lambda e: (jnp.minimum(e, last), 0, 0))] * 2,
        out_specs=pl.BlockSpec((32, 32 * group, LANES), lambda e: (0, e, 0)),
        out_shape=jax.ShapeDtypeStruct((32, 32 * (experts + 1), LANES), jnp.bfloat16),
        scratch_shapes=[pltpu.VMEM((LANES, columns), jnp.float32)],
        compiler_params=pltpu.CompilerParams(vmem_limit_bytes=60 << 20),
    )(w_gate, w_up)


def decode_kernel(got_ref, stats_ref, gate_ref, up_ref, gate_scale_ref, up_scale_ref, factor_ref, value_ref, *, experts, group):
    step = pl.program_id(0)

    @pl.when(step == 0)
    def _():
        stats = stats_ref[...].astype(jnp.float32)
        total = jnp.sum(stats, axis=0)
        total = pltpu.roll(total, LANES - 2 * experts, 1) + pltpu.roll(total, LANES - 4 * experts, 1)
        scale = total / D_MODEL
        factor_ref[...] = stats * (1.0 / (SPAN * LN2)) / scale[None]
        turned = jnp.concatenate([scale] * 4, axis=0).T
        gate_scale_ref[...] = turned[:experts, :32]
        up_scale_ref[...] = turned[experts : 2 * experts, :32]

    to = lax.broadcasted_iota(jnp.int32, (2 * LANES, 2 * LANES), 1)
    of = lax.broadcasted_iota(jnp.int32, (2 * LANES, 2 * LANES), 0)
    move = of == to % 64 + to // 64 % 2 * LANES + to // LANES * 64
    move = jnp.where(move, 1.0, 0.0).astype(jnp.bfloat16)

    def one(i, _):
        e = step * group + i
        row = pl.multiple_of(i * 32, 32)
        which = jnp.where(lax.broadcasted_iota(jnp.int32, (32, LANES), 1) < 64, e, experts + e)
        for s in range(32):
            code = got_ref[s, pl.ds(row, 32)].astype(jnp.float32)
            factor = jnp.take_along_axis(factor_ref[s], which, axis=1)
            size = (jnp.log(jnp.abs(code)) + SPAN / 2 * LN2) * factor
            value = jnp.where(code < 0, -size, size).astype(jnp.bfloat16)
            value_ref[i, s // 2 * 32 : s // 2 * 32 + 32, s % 2 * LANES : (s % 2 + 1) * LANES] = value
        both = jnp.dot(value_ref[i], move, preferred_element_type=jnp.float32).astype(jnp.bfloat16)
        for p in range(16):
            gate_ref[i, :, p * LANES : (p + 1) * LANES] = both[p * 32 : (p + 1) * 32, :LANES]
            up_ref[i, :, p * LANES : (p + 1) * LANES] = both[p * 32 : (p + 1) * 32, LANES:]

    lax.fori_loop(0, group, one, None, unroll=UNROLL)


def decode(got, experts):
    out = jax.ShapeDtypeStruct((experts, 32, D_MODEL), jnp.bfloat16)
    scale = jax.ShapeDtypeStruct((experts, 32), jnp.float32)
    group = GROUP
    return pl.pallas_call(
        lambda *refs: decode_kernel(*refs, experts=experts, group=group),
        name="decode",
        grid=(experts // group,),
        in_specs=[
            pl.BlockSpec((32, 32 * group, LANES), lambda e: (0, e, 0)),
            pl.BlockSpec((32, 32, LANES), lambda e: (0, experts, 0)),
        ],
        out_specs=[pl.BlockSpec((group, 32, D_MODEL), lambda e: (e, 0, 0))] * 2
        + [pl.BlockSpec((experts, 32), lambda e: (0, 0))] * 2,
        out_shape=[out, out, scale, scale],
        scratch_shapes=[pltpu.VMEM((32, 32, LANES), jnp.float32), pltpu.VMEM((group, 512, 2 * LANES), jnp.bfloat16)],
        compiler_params=pltpu.CompilerParams(vmem_limit_bytes=60 << 20),
    )(got, got)


def sent_to_all(array, axis):
    count = lax.axis_size(axis)
    return lax.all_to_all(jnp.broadcast_to(array[None], (count, *array.shape)), axis, 0, 0, tiled=True)


def joined(array, axis):
    count, me = lax.axis_size(axis), lax.axis_index(axis)
    near = [array] + [lax.ppermute(array, axis, [(s, (s + k) % count) for s in range(count)]) for k in range(1, count)]
    ring = jnp.concatenate((near[::-1] * 2)[: 2 * count - 1])
    return lax.dynamic_slice_in_dim(ring, (count - 1 - me) * len(array), count * len(array))


def local(w_gate, w_up, router_weight, router_gain):
    router = (router_weight * router_gain[:, None]).astype(jnp.bfloat16).T
    router = jnp.moveaxis(sent_to_all(router, "zero"), 0, 1).reshape(router.shape[0], D_MODEL)
    router = joined(router, "bank").T
    sent = encode(w_gate, w_up)
    got = lax.all_to_all(sent, "zero", 0, 0, tiled=True)
    gate, up, scale_gate, scale_up = decode(got, w_gate.shape[0])
    return jnp.swapaxes(gate, 1, 2), jnp.swapaxes(up, 1, 2), scale_gate, scale_up, router


def solution(mesh):
    placed = (
        P(("trial", "bank"), "zero", None),
        P(("trial", "bank"), "zero", None),
        P(("trial", "zero"), "bank"),
        P(("trial", "zero")),
    )
    return jax.shard_map(
        local,
        mesh=mesh,
        in_specs=placed,
        out_specs=(
            P(("trial", "bank"), None, "zero"),
            P(("trial", "bank"), None, "zero"),
            P(("trial", "bank"), "zero"),
            P(("trial", "bank"), "zero"),
            P("trial", None),
        ),
        check_vma=False,
    )
```

time: 198 us -> 141 us (0.71)
  Pallas kernels: 63.1 us -> 16 us
  blocking collectives: 20.2 us -> 0 us
  starting transfers between devices: 10.8 us -> 25.7 us
  waiting for transfers between devices: 97.9 us -> 93.2 us
    pallas_call x1, Pallas kernels: 49.8 us -> 8.05 us  [decode(): pl.pallas_call(lambda *refs: decode_kernel(*refs, experts=experts, group=...]
    all_to_all x1 -> x0, blocking collectives: 20.2 us -> none  [sent_to_all(): lax.all_to_all(jnp.broadcast_to(array[None], (count, *array.shape)), axis...]
    all_to_all x1, waiting for transfers between devices: 97.9 us -> 90.1 us  [local(): got = lax.all_to_all(sent, 'zero', 0, 0, tiled=True)]
    all_to_all x1, starting transfers between devices: 4.82 us -> 11.7 us  [sent_to_all(): lax.all_to_all(jnp.broadcast_to(array[None], (count, *array.shape)), axis...]
    pallas_call x1, Pallas kernels: 13.3 us -> 7.99 us  [encode(): pl.pallas_call(lambda *refs: encode_kernel(*refs, experts=experts, bands=...]
    ppermute x0 -> x3, starting transfers between devices: none -> 4.83 us  [joined(): lax.ppermute(array, axis, [(s, (s + k) % count) for s in range(count)])]
    all_to_all x1, starting transfers between devices: 5.96 us -> 9.13 us  [local(): got = lax.all_to_all(sent, 'zero', 0, 0, tiled=True)]
    ppermute x0 -> x3, waiting for transfers between devices: none -> 2.45 us  [joined(): lax.ppermute(array, axis, [(s, (s + k) % count) for s in range(count)])]
  transfers between devices with their start and end apart: 2 -> 5, of which waited for: 1 -> 4; matrix products, arithmetic and copies ran while one was open for 0% -> 1% of each run, Pallas kernels for 7% -> 6%
where the time goes in v2:
time: 141 us; the launch traced here: 138 us
  waiting for transfers between devices  93.2 us (66%)
  starting transfers between devices  25.7 us (18%)
  Pallas kernels  16 us (11%)
  local copies, waits for them, and re-layouts  1.91 us (1%)
    all_to_all x1, waiting for transfers between devices, local(): got = lax.all_to_all(sent, 'zero', 0, 0, tiled=True)  90.1 us
    all_to_all x1, starting transfers between devices, sent_to_all(): lax.all_to_all(jnp.broadcast_to(array[None], (count, *array.shape)), axis...  11.7 us
    all_to_all x1, starting transfers between devices, local(): got = lax.all_to_all(sent, 'zero', 0, 0, tiled=True)  9.13 us
    pallas_call x1, Pallas kernels, decode(): pl.pallas_call(lambda *refs: decode_kernel(*refs, experts=experts, group=...  8.05 us
    pallas_call x1, Pallas kernels, encode(): pl.pallas_call(lambda *refs: encode_kernel(*refs, experts=experts, bands=...  7.99 us
    ppermute x3, starting transfers between devices, joined(): lax.ppermute(array, axis, [(s, (s + k) % count) for s in range(count)])  4.83 us
  transfers between devices with their start and end apart: 5, of which 4 were waited for; matrix products, arithmetic and copies ran while one was open for 1% of the time, Pallas kernels for 6%

profile of v2, /device:TPU:10, one launch (start us, length us, event | category | flops | bytes accessed | tf_op | source)
XLA Modules:
  0.0 138.3 jit_solution(18323308782246181853)
XLA Ops:
  0.6 0.7 fusion
  1.4 0.8 reshape.16
  2.1 11.7 %all-to-all-start.1 = ((bf16[32,2,512]{2,1,0:T(2,128)(2,1)}), bf16[32,2,512]{2,1,0:T(2,128)(2,1)S(1)}, u32[]{:S(2)}, u32[]{:S(2)}) async-start(bf16[32,2,512]{2,1,0:T(2,128)(2,1)} %reshape.16), calls=%async_computation.1 | async-start | bytes 131072 | tf_op jit(solution)/shard_map/all_to_all | solution.py:134
  13.8 8.0 %encode.1 = bf16[32,544,128]{2,1,0:T(8,128)(2,1)} custom-call(f32[16,64,1024]{2,1,0:T(8,128)} %refs_0_.1, f32[16,64,1024]{2,1,0:T(8,128)} %refs_1_.1), custom_call_target="tpu_custom_call" | custom-call | tf_op jit(solution)/shard_map/encode/pallas_call | solution.py:63
  21.8 0.7 all-to-all-done.1
  22.5 9.1 %all-to-all-start = ((bf16[32,544,128]{2,1,0:T(8,128)(2,1)}), bf16[32,544,128]{2,1,0:T(8,128)(2,1)}, u32[]{:S(2)}, u32[]{:S(2)}) async-start(bf16[32,544,128]{2,1,0:T(8,128)(2,1)} %encode.1), calls=%async_computation | async-start | bytes 8912896 | tf_op jit(solution)/shard_map/all_to_all | solution.py:149
  31.7 0.1 reshape.17
  31.8 0.2 reshape.15
  32.0 0.6 collective-permute-start
  32.6 2.4 %collective-permute-start.1 = (bf16[16,2048]{1,0:T(8,128)(2,1)S(1)}, bf16[16,2048]{1,0:T(8,128)(2,1)S(1)}, u32[]{:S(2)}, u32[]{:S(2)}) collective-permute-start(bf16[16,2048]{1,0:T(8,128)(2,1)S(1)} %reshape.15), channel_id=1, source_target_pairs={{0,64},{32,96},{64,0},{96,32},{1,65},{33,97},{65,1},{97,33},{2,66}... | collective-permute-start | bytes 196616 | tf_op jit(solution)/shard_map/ppermute | solution.py:139
  35.1 1.8 %collective-permute-start.2 = (bf16[16,2048]{1,0:T(8,128)(2,1)S(1)}, bf16[16,2048]{1,0:T(8,128)(2,1)S(1)}, u32[]{:S(2)}, u32[]{:S(2)}) collective-permute-start(bf16[16,2048]{1,0:T(8,128)(2,1)S(1)} %reshape.15), channel_id=1, source_target_pairs={{0,32},{32,64},{64,96},{96,0},{1,33},{33,65},{65,97},{97,1},{2,34}... | collective-permute-start | bytes 196616 | tf_op jit(solution)/shard_map/ppermute | solution.py:139
  36.9 0.0 collective-permute-done
  36.9 1.5 %collective-permute-done.1 = bf16[16,2048]{1,0:T(8,128)(2,1)S(1)} collective-permute-done((bf16[16,2048]{1,0:T(8,128)(2,1)S(1)}, bf16[16,2048]{1,0:T(8,128)(2,1)S(1)}, u32[]{:S(2)}, u32[]{:S(2)}) %collective-permute-start.1) | collective-permute-done | bytes 65568 | tf_op jit(solution)/shard_map/ppermute | solution.py:139
  38.4 0.9 collective-permute-done.2
  39.4 0.7 dynamic-slice_bitcast_fusion
  40.1 90.1 %all-to-all-done.refs_0_.refs_1_ = bf16[32,544,128]{2,1,0:T(8,128)(2,1)} async-done(((bf16[32,544,128]{2,1,0:T(8,128)(2,1)}), bf16[32,544,128]{2,1,0:T(8,128)(2,1)}, u32[]{:S(2)}, u32[]{:S(2)}) %all-to-all-start) | async-done | bytes 4456480 | tf_op jit(solution)/shard_map/all_to_all | solution.py:149
  130.2 8.1 %decode.1 = (bf16[16,32,2048]{2,1,0:T(8,128)(2,1)}, bf16[16,32,2048]{2,1,0:T(8,128)(2,1)}, f32[16,32]{1,0:T(8,128)}, f32[16,32]{1,0:T(8,128)}) custom-call(bf16[32,544,128]{2,1,0:T(8,128)(2,1)} %all-to-all-done.refs_0_.refs_1_, bf16[32,544,128]{2,1,0:T(8,128)(2,1)} %all-to-all-done.refs_0_.refs_1_), custom_call_target="tpu_custom_call" | custom-call | tf_op jit(solution)/shard_map/decode/pallas_call | solution.py:116
  (9 shorter events, 0.1 us)
Async XLA Ops:
  2.1 20.4 %all-to-all-start.1 = ((bf16[32,2,512]{2,1,0:T(2,128)(2,1)}), bf16[32,2,512]{2,1,0:T(2,128)(2,1)S(1)}, u32[]{:S(2)}, u32[]{:S(2)}) async-start(bf16[32,2,512]{2,1,0:T(2,128)(2,1)} %reshape.16), calls=%async_computation.1 | async-start | bytes 131072 | tf_op jit(solution)/shard_map/all_to_all | solution.py:134
  22.5 107.7 %all-to-all-start = ((bf16[32,544,128]{2,1,0:T(8,128)(2,1)}), bf16[32,544,128]{2,1,0:T(8,128)(2,1)}, u32[]{:S(2)}, u32[]{:S(2)}) async-start(bf16[32,544,128]{2,1,0:T(8,128)(2,1)} %encode.1), calls=%async_computation | async-start | bytes 8912896 | tf_op jit(solution)/shard_map/all_to_all | solution.py:149
  32.0 4.8 %collective-permute-start = (bf16[16,2048]{1,0:T(8,128)(2,1)S(1)}, bf16[16,2048]{1,0:T(8,128)(2,1)S(1)}, u32[]{:S(2)}, u32[]{:S(2)}) collective-permute-start(bf16[16,2048]{1,0:T(8,128)(2,1)S(1)} %reshape.15), channel_id=1, source_target_pairs={{0,96},{32,0},{64,32},{96,64},{1,97},{33,1},{65,33},{97,65},{2,98}... | collective-permute-start | bytes 196616 | tf_op jit(solution)/shard_map/ppermute | solution.py:139
  32.6 5.8 %collective-permute-start.1 = (bf16[16,2048]{1,0:T(8,128)(2,1)S(1)}, bf16[16,2048]{1,0:T(8,128)(2,1)S(1)}, u32[]{:S(2)}, u32[]{:S(2)}) collective-permute-start(bf16[16,2048]{1,0:T(8,128)(2,1)S(1)} %reshape.15), channel_id=1, source_target_pairs={{0,64},{32,96},{64,0},{96,32},{1,65},{33,97},{65,1},{97,33},{2,66}... | collective-permute-start | bytes 196616 | tf_op jit(solution)/shard_map/ppermute | solution.py:139
  35.1 4.3 %collective-permute-start.2 = (bf16[16,2048]{1,0:T(8,128)(2,1)S(1)}, bf16[16,2048]{1,0:T(8,128)(2,1)S(1)}, u32[]{:S(2)}, u32[]{:S(2)}) collective-permute-start(bf16[16,2048]{1,0:T(8,128)(2,1)S(1)} %reshape.15), channel_id=1, source_target_pairs={{0,32},{32,64},{64,96},{96,0},{1,33},{33,65},{65,97},{97,1},{2,34}... | collective-permute-start | bytes 196616 | tf_op jit(solution)/shard_map/ppermute | solution.py:139

commit v3 on v1

v3 whole, which is shorter than its diff:
```python
import jax
import jax.numpy as jnp
from jax import lax
from jax.experimental import pallas as pl
from jax.experimental.pallas import tpu as pltpu
from jax.sharding import PartitionSpec as P

D_MODEL = 2048
LANES = 128
SPAN = 126.0
LN2 = 0.6931471805599453
GROUP = 4
DEEP, WIDE = 8, 4
ALL = pltpu.CompilerParams(vmem_limit_bytes=60 << 20)
SOME = pltpu.CompilerParams(vmem_limit_bytes=24 << 20)


def measured(w):
    size = jnp.abs(w)
    total = jnp.sum(size, axis=0, keepdims=True)
    top = jnp.max(size, axis=0, keepdims=True)
    return total, (top * (1 + 2.0**-7)).astype(jnp.bfloat16).astype(jnp.float32)


def coded(w, top):
    return jnp.exp2(w * jnp.where(top > 1e-30, SPAN / jnp.maximum(top, 1e-30), 0.0))


def turned(gate, up, gate_top, up_top):
    return jnp.concatenate([coded(gate, gate_top), coded(up, up_top)], axis=0).T.astype(jnp.bfloat16)


def encode_kernel(gate_ref, up_ref, router_ref, gain_ref, out_ref, stats_ref, *, experts, bands):
    step = pl.program_id(0)
    groups = experts // GROUP

    def one(i, code):
        e = step * GROUP + i
        row = pl.multiple_of(i * 32, 32)
        kept = []
        for t in range(bands):
            lanes = slice(t * LANES, (t + 1) * LANES)
            gate, up = gate_ref[i, :, lanes], up_ref[i, :, lanes]
            gate_total, gate_top = measured(gate)
            up_total, up_top = measured(up)
            gate_high, up_high = (v.astype(jnp.bfloat16).astype(jnp.float32) for v in (gate_total, up_total))
            kept.append((gate_top, up_top, gate_high, up_high, gate_total - gate_high, up_total - up_high))
            if code:
                tile = turned(gate, up, gate_top, up_top)
                for y in range(WIDE):
                    out_ref[WIDE * t + y, pl.ds(row, 32)] = tile[32 * y : 32 * (y + 1)]
        for k, parts in enumerate(zip(*kept)):
            stats_ref[pl.ds(k * experts + e, 1)] = jnp.concatenate(parts, axis=1)

    @pl.when(step < groups - 1)
    def _():
        lax.fori_loop(0, GROUP, lambda i, _: one(i, True), None, unroll=2)

    @pl.when(step == groups - 1)
    def _():
        lax.fori_loop(0, GROUP, lambda i, _: one(i, False), None, unroll=2)
        router = (router_ref[...] * gain_ref[...]).astype(jnp.bfloat16).astype(jnp.float32)
        router = jnp.concatenate([router[:, :32], router[:, 32:]], axis=0)
        router = jnp.concatenate([router] * 4, axis=1)
        for t in range(bands):
            stats_ref[6 * experts :, t * LANES : (t + 1) * LANES] = router
        for t in range(bands):
            tile = stats_ref[:, t * LANES : (t + 1) * LANES].T.astype(jnp.bfloat16)
            for y in range(WIDE):
                out_ref[WIDE * t + y, :32] = tile[32 * y : 32 * (y + 1)]


def encode(w_gate, w_up, router, gain):
    experts, rows, columns = w_gate.shape
    groups = experts // GROUP
    return pl.pallas_call(
        lambda *refs: encode_kernel(*refs, experts=experts, bands=columns // LANES),
        name="encode",
        grid=(groups,),
        in_specs=[pl.BlockSpec((GROUP, rows, columns), lambda g: (g, 0, 0))] * 2
        + [pl.BlockSpec(router.shape, lambda g: (0, 0)), pl.BlockSpec(gain.shape, lambda g: (0, 0))],
        out_specs=pl.BlockSpec((32, 32 * GROUP, LANES), lambda g: (0, g, 0)),
        out_shape=jax.ShapeDtypeStruct((32, 32 * (experts - GROUP + 1), LANES), jnp.bfloat16),
        scratch_shapes=[pltpu.VMEM((LANES, columns), jnp.float32)],
        compiler_params=ALL,
    )(w_gate, w_up, router, gain)


def encode_rest_kernel(at_ref, gate_ref, up_ref, out_ref, *, bands):
    z, y = at_ref[0], at_ref[1]

    def one(i, _):
        row = pl.multiple_of(i * 32, 32)
        for t in range(bands):
            lanes = slice(t * LANES, (t + 1) * LANES)
            gate, up = gate_ref[i, :, lanes], up_ref[i, :, lanes]
            tile = turned(gate, up, measured(gate)[1], measured(up)[1])
            for k in range(WIDE):
                to = (k - y) % WIDE * DEEP + (t - z) % DEEP
                out_ref[to, pl.ds(row, 32)] = tile[32 * k : 32 * (k + 1)]

    lax.fori_loop(0, GROUP, one, None, unroll=2)


def encode_rest(at, w_gate, w_up):
    experts, rows, columns = w_gate.shape
    return pl.pallas_call(
        lambda *refs: encode_rest_kernel(*refs, bands=columns // LANES),
        name="encode_rest",
        grid_spec=pltpu.PrefetchScalarGridSpec(
            num_scalar_prefetch=1,
            grid=(1,),
            in_specs=[pl.BlockSpec((GROUP, rows, columns), lambda _, at: (experts // GROUP - 1, 0, 0))] * 2,
            out_specs=pl.BlockSpec((32, 32 * GROUP, LANES), lambda _, at: (0, 0, 0)),
        ),
        out_shape=jax.ShapeDtypeStruct((32, 32 * GROUP, LANES), jnp.bfloat16),
        compiler_params=ALL,
    )(at, w_gate, w_up)


def unpack_kernel(stats_ref, factor_ref, gate_scale_ref, up_scale_ref, router_ref, *, experts):
    stats = stats_ref[...].astype(jnp.float32)
    total = jnp.sum(stats, axis=0)
    total = pltpu.roll(total, LANES - 2 * experts, 1) + pltpu.roll(total, LANES - 4 * experts, 1)
    scale = total / D_MODEL
    lane = lax.broadcasted_iota(jnp.int32, (32, LANES), 1)
    factor_ref[...] = jnp.where(lane < 2 * experts, stats / (SPAN * LN2) / scale, 0.0)
    scale = jnp.concatenate([scale] * 4, axis=0).T
    gate_scale_ref[...] = scale[:experts, :32]
    up_scale_ref[...] = scale[experts : 2 * experts, :32]
    to = lax.broadcasted_iota(jnp.int32, (2 * LANES, 2 * LANES), 1)
    of = lax.broadcasted_iota(jnp.int32, (2 * LANES, 2 * LANES), 0)
    move = jnp.where(of == to % 32 + to // 64 * 32 + to // 32 % 2 * LANES, 1.0, 0.0).astype(jnp.bfloat16)
    for q in range(DEEP):
        part = stats[4 * q : 4 * (q + 1)].reshape(LANES, LANES).T[6 * experts :].astype(jnp.bfloat16)
        part = jnp.concatenate([part[: len(part) // 2], part[len(part) // 2 :]], axis=1)
        part = jnp.dot(part, move, preferred_element_type=jnp.float32)
        router_ref[:, 2 * LANES * q : 2 * LANES * (q + 1)] = part.astype(jnp.bfloat16)


def unpack(got, experts):
    scale = jax.ShapeDtypeStruct((experts, 32), jnp.float32)
    whole = lambda shape: pl.BlockSpec(shape, lambda _: (0,) * len(shape))
    return pl.pallas_call(
        lambda *refs: unpack_kernel(*refs, experts=experts),
        name="unpack",
        grid=(1,),
        in_specs=[pl.BlockSpec((32, 32, LANES), lambda _: (0, experts - GROUP, 0))],
        out_specs=[whole((32, 32, LANES)), whole((experts, 32)), whole((experts, 32)), whole((16, D_MODEL))],
        out_shape=[
            jax.ShapeDtypeStruct((32, 32, LANES), jnp.float32),
            scale,
            scale,
            jax.ShapeDtypeStruct((16, D_MODEL), jnp.bfloat16),
        ],
        compiler_params=SOME,
    )(got)


def decoded(read, factor_ref, gate_ref, up_ref, value_ref, experts, first):
    to = lax.broadcasted_iota(jnp.int32, (2 * LANES, 2 * LANES), 1)
    of = lax.broadcasted_iota(jnp.int32, (2 * LANES, 2 * LANES), 0)
    move = of == to % 64 + to // 64 % 2 * LANES + to // LANES * 64
    move = jnp.where(move, 1.0, 0.0).astype(jnp.bfloat16)

    def one(i, _):
        row = pl.multiple_of(i * 32, 32)
        e = first + i
        which = jnp.where(lax.broadcasted_iota(jnp.int32, (32, LANES), 1) < 64, e, experts + e)
        for s in range(32):
            factor = jnp.take_along_axis(factor_ref[s], which, axis=1)
            value = (jnp.log(read(s, row).astype(jnp.float32)) * factor).astype(jnp.bfloat16)
            value_ref[i, s // 2 * 32 : s // 2 * 32 + 32, s % 2 * LANES : (s % 2 + 1) * LANES] = value
        both = jnp.dot(value_ref[i], move, preferred_element_type=jnp.float32).astype(jnp.bfloat16)
        for p in range(16):
            gate_ref[i, :, p * LANES : (p + 1) * LANES] = both[p * 32 : (p + 1) * 32, :LANES]
            up_ref[i, :, p * LANES : (p + 1) * LANES] = both[p * 32 : (p + 1) * 32, LANES:]

    lax.fori_loop(0, GROUP, one, None, unroll=2)


def decode_kernel(got_ref, factor_ref, gate_ref, up_ref, value_ref, *, experts):
    read = lambda s, row: got_ref[s, pl.ds(row, 32)]
    decoded(read, factor_ref, gate_ref, up_ref, value_ref, experts, pl.program_id(0) * GROUP)


def decode(got, factor, experts):
    out = jax.ShapeDtypeStruct((experts, 32, D_MODEL), jnp.bfloat16)
    return pl.pallas_call(
        lambda *refs: decode_kernel(*refs, experts=experts),
        name="decode",
        grid=(experts // GROUP - 1,),
        in_specs=[
            pl.BlockSpec((32, 32 * GROUP, LANES), lambda g: (0, g, 0)),
            pl.BlockSpec((32, 32, LANES), lambda g: (0, 0, 0)),
        ],
        out_specs=[pl.BlockSpec((GROUP, 32, D_MODEL), lambda g: (g, 0, 0))] * 2,
        out_shape=[out, out],
        scratch_shapes=[pltpu.VMEM((GROUP, 512, 2 * LANES), jnp.bfloat16)],
        compiler_params=SOME,
    )(got, factor)


def decode_rest_kernel(at_ref, *refs, experts):
    parts, (factor_ref, _, _, gate_ref, up_ref, got_ref, value_ref) = refs[:DEEP], refs[DEEP:]
    z, y = at_ref[0], at_ref[1]
    for k, part in enumerate(parts):
        for j in range(WIDE):
            got_ref[(z - k) % DEEP * WIDE + (y - j) % WIDE] = part[j]
    read = lambda s, row: got_ref[s, pl.ds(row, 32)]
    decoded(read, factor_ref, gate_ref, up_ref, value_ref, experts, experts - GROUP)


def decode_rest(at, parts, factor, gate, up):
    experts = gate.shape[0]
    last = experts // GROUP - 1
    return pl.pallas_call(
        lambda *refs: decode_rest_kernel(*refs, experts=experts),
        name="decode_rest",
        grid_spec=pltpu.PrefetchScalarGridSpec(
            num_scalar_prefetch=1,
            grid=(1,),
            in_specs=[pl.BlockSpec(parts[0].shape, lambda _, at: (0, 0, 0))] * DEEP
            + [pl.BlockSpec((32, 32, LANES), lambda _, at: (0, 0, 0))]
            + [pl.BlockSpec(memory_space=pl.ANY)] * 2,
            out_specs=[pl.BlockSpec((GROUP, 32, D_MODEL), lambda _, at: (last, 0, 0))] * 2,
            scratch_shapes=[
                pltpu.VMEM((32, 32 * GROUP, LANES), jnp.bfloat16),
                pltpu.VMEM((GROUP, 512, 2 * LANES), jnp.bfloat16),
            ],
        ),
        out_shape=[jax.ShapeDtypeStruct(gate.shape, gate.dtype)] * 2,
        input_output_aliases={DEEP + 2: 0, DEEP + 3: 1},
        compiler_params=SOME,
    )(at, *parts, factor, gate, up)


def joined(array, axis):
    count, me = lax.axis_size(axis), lax.axis_index(axis)
    near = [array] + [lax.ppermute(array, axis, [(s, (s + k) % count) for s in range(count)]) for k in range(1, count)]
    ring = jnp.concatenate((near[::-1] * 2)[: 2 * count - 1])
    return lax.dynamic_slice_in_dim(ring, (count - 1 - me) * len(array), count * len(array))


def offset(array, deep, wide):
    pairs = []
    for s in range(DEEP * WIDE):
        z, y = divmod(s, WIDE)
        pairs.append((s, (z + deep) % DEEP * WIDE + (y + wide) % WIDE))
    return lax.ppermute(array, "zero", pairs)


def local(w_gate, w_up, router_weight, router_gain):
    experts = w_gate.shape[0]
    me = lax.axis_index("zero")
    at = jnp.stack([me // WIDE, me % WIDE]).astype(jnp.int32)
    sent = encode(w_gate, w_up, router_weight.T, router_gain[None])
    got = lax.all_to_all(sent, "zero", 0, 0, tiled=True)
    rest = encode_rest(at, w_gate, w_up)
    rows = [rest[:DEEP]]
    for k in range(1, WIDE):
        rows.append(offset(rest[DEEP * k : DEEP * (k + 1)], 0, k))
    parts = [jnp.stack([row[k] for row in rows]) for k in range(DEEP)]
    for k in range(1, DEEP):
        parts[k] = offset(parts[k], k, 0)
    factor, scale_gate, scale_up, router = unpack(got, experts)
    gate, up = decode(got, factor, experts)
    router = joined(router, "bank").T
    gate, up = decode_rest(at, parts, factor, gate, up)
    return jnp.swapaxes(gate, 1, 2), jnp.swapaxes(up, 1, 2), scale_gate, scale_up, router


def solution(mesh):
    placed = (
        P(("trial", "bank"), "zero", None),
        P(("trial", "bank"), "zero", None),
        P(("trial", "zero"), "bank"),
        P(("trial", "zero")),
    )
    return jax.shard_map(
        local,
        mesh=mesh,
        in_specs=placed,
        out_specs=(
            P(("trial", "bank"), None, "zero"),
            P(("trial", "bank"), None, "zero"),
            P(("trial", "bank"), "zero"),
            P(("trial", "bank"), "zero"),
            P("trial", None),
        ),
        check_vma=False,
    )
```

time: 198 us -> 131 us (0.66)
  the two profiles are of different devices: /device:TPU:10 before, /device:TPU:96 now
where the time goes in v3:
time: 131 us
  waiting for transfers between devices  62.5 us (48%)
  starting transfers between devices  37.1 us (28%)
  Pallas kernels  20.7 us (16%)
  local copies, waits for them, and re-layouts  5.98 us (5%)
  other arithmetic  4.02 us (3%)
    ppermute x10, waiting for transfers between devices, offset(): return lax.ppermute(array, 'zero', pairs)  61.7 us
    ppermute x10, starting transfers between devices, offset(): return lax.ppermute(array, 'zero', pairs)  22.2 us
    all_to_all x1, starting transfers between devices, local(): got = lax.all_to_all(sent, 'zero', 0, 0, tiled=True)  10.5 us
    pallas_call x1, Pallas kernels, encode(): pl.pallas_call(lambda *refs: encode_kernel(*refs, experts=experts, bands=...  6.93 us
    pallas_call x1, Pallas kernels, decode(): pl.pallas_call(lambda *refs: decode_kernel(*refs, experts=experts), name=...  5.19 us
    ppermute x3, starting transfers between devices, joined(): lax.ppermute(array, axis, [(s, (s + k) % count) for s in range(count)])  4.45 us
    pallas_call x1, Pallas kernels, decode_rest(): pl.pallas_call(lambda *refs: decode_rest_kernel(*refs, experts=experts),...  3.89 us
    pallas_call x1, Pallas kernels, encode_rest(): pl.pallas_call(lambda *refs: encode_rest_kernel(*refs, bands=columns // L...  3.75 us
  transfers between devices with their start and end apart: 14, of which 6 were waited for; matrix products, arithmetic and copies ran while one was open for 7% of the time, Pallas kernels for 11%

profile of v3, /device:TPU:96, one launch (start us, length us, event | category | flops | bytes accessed | tf_op | source)
XLA Modules:
  0.0 131.0 jit_solution(17284054070250775236)
XLA Ops:
  0.6 6.9 %encode.1 = bf16[32,416,128]{2,1,0:T(8,128)(2,1)} custom-call(f32[16,64,1024]{2,1,0:T(8,128)} %refs_0_.1, f32[16,64,1024]{2,1,0:T(8,128)} %refs_1_.3, f32[16,64]{1,0:T(8,128)} %bitcast.10, f32[1,64]{1,0:T(1,128)} %bitcast.11), custom_call_target="tpu_custom_call" | custom-call | tf_op jit(solution)/shard_map/encode/pallas_call | solution.py:76
  7.6 10.5 %all-to-all-start = ((bf16[32,416,128]{2,1,0:T(8,128)(2,1)}), bf16[32,416,128]{2,1,0:T(8,128)(2,1)S(1)}, u32[]{:S(2)}, u32[]{:S(2)}) async-start(bf16[32,416,128]{2,1,0:T(8,128)(2,1)} %encode.1), calls=%async_computation | async-start | bytes 6815744 | tf_op jit(solution)/shard_map/all_to_all | solution.py:258
  18.7 3.8 %encode_rest.1 = bf16[32,128,128]{2,1,0:T(8,128)(2,1)} custom-call(s32[2]{0:T(128)} %pad_add_fusion.refs_0_, f32[16,64,1024]{2,1,0:T(8,128)} %refs_0_.1, f32[16,64,1024]{2,1,0:T(8,128)} %refs_1_.3), custom_call_target="tpu_custom_call" | custom-call | tf_op jit(solution)/shard_map/encode_rest/pallas_call | solution.py:107
  22.4 1.2 fusion.1
  23.6 1.5 %collective-permute-start = (bf16[8,128,128]{2,1,0:T(8,128)(2,1)S(1)}, bf16[8,128,128]{2,1,0:T(8,128)(2,1)S(1)}, u32[]{:S(2)}, u32[]{:S(2)}) collective-permute-start(bf16[8,128,128]{2,1,0:T(8,128)(2,1)S(1)} %get-tuple-element.29), channel_id=1, source_target_pairs={{0,1},{1,2},{2,3},{3,0},{4,5},{5,6},{6,7},{7,4},{8,9},{9,10},{10,1... | collective-permute-start | bytes 786440 | tf_op jit(solution)/shard_map/ppermute | solution.py:250
  25.1 2.7 %collective-permute-start.1 = (bf16[8,128,128]{2,1,0:T(8,128)(2,1)S(1)}, bf16[8,128,128]{2,1,0:T(8,128)(2,1)S(1)}, u32[]{:S(2)}, u32[]{:S(2)}) collective-permute-start(bf16[8,128,128]{2,1,0:T(8,128)(2,1)S(1)} %get-tuple-element.31), channel_id=1, source_target_pairs={{0,2},{1,3},{2,0},{3,1},{4,6},{5,7},{6,4},{7,5},{8,10},{9,11},{10,... | collective-permute-start | bytes 786440 | tf_op jit(solution)/shard_map/ppermute | solution.py:250
  27.8 1.5 %collective-permute-start.2 = (bf16[8,128,128]{2,1,0:T(8,128)(2,1)S(1)}, bf16[8,128,128]{2,1,0:T(8,128)(2,1)S(1)}, u32[]{:S(2)}, u32[]{:S(2)}) collective-permute-start(bf16[8,128,128]{2,1,0:T(8,128)(2,1)S(1)} %get-tuple-element.30), channel_id=1, source_target_pairs={{0,3},{1,0},{2,1},{3,2},{4,7},{5,4},{6,5},{7,6},{8,11},{9,8},{10,9... | collective-permute-start | bytes 786440 | tf_op jit(solution)/shard_map/ppermute | solution.py:250
  29.3 1.5 %fusion = (bf16[1,128,128]{2,1,0:T(8,128)(2,1)S(1)}, bf16[1,128,128]{2,1,0:T(8,128)(2,1)S(1)}, bf16[1,128,128]{2,1,0:T(8,128)(2,1)S(1)}, bf16[1,128,128]{2,1,0:T...) fusion(bf16[32,128,128]{2,1,0:T(8,128)(2,1)} %encode_rest.1), kind=kLoop, calls=%fused_computation.17 | loop fusion | bytes 524288 | tf_op jit(solution)/shard_map/slice | solution.py:263
  30.8 22.4 %collective-permute-done = bf16[8,128,128]{2,1,0:T(8,128)(2,1)S(1)} collective-permute-done((bf16[8,128,128]{2,1,0:T(8,128)(2,1)S(1)}, bf16[8,128,128]{2,1,0:T(8,128)(2,1)S(1)}, u32[]{:S(2)}, u32[]{:S(2)}) %collective-permute-start) | collective-permute-done | bytes 262176 | tf_op jit(solution)/shard_map/ppermute | solution.py:250
  55.0 1.7 %collective-permute-start.9 = (bf16[4,128,128]{2,1,0:T(8,128)(2,1)S(1)}, bf16[4,128,128]{2,1,0:T(8,128)(2,1)S(1)}, u32[]{:S(2)}, u32[]{:S(2)}) collective-permute-start(bf16[4,128,128]{2,1,0:T(8,128)(2,1)S(1)} %pad_maximum_fusion.7), channel_id=1, source_target_pairs={{0,28},{1,29},{2,30},{3,31},{4,0},{5,1},{6,2},{7,3},{8,4},{9,5},{1... | collective-permute-start | bytes 393224 | tf_op jit(solution)/shard_map/ppermute | solution.py:250
  56.8 1.3 %collective-permute-start.8 = (bf16[4,128,128]{2,1,0:T(8,128)(2,1)S(1)}, bf16[4,128,128]{2,1,0:T(8,128)(2,1)S(1)}, u32[]{:S(2)}, u32[]{:S(2)}) collective-permute-start(bf16[4,128,128]{2,1,0:T(8,128)(2,1)S(1)} %pad_maximum_fusion.6), channel_id=1, source_target_pairs={{0,24},{1,25},{2,26},{3,27},{4,28},{5,29},{6,30},{7,31},{8,0},{9,1... | collective-permute-start | bytes 393224 | tf_op jit(solution)/shard_map/ppermute | solution.py:250
  58.1 0.7 pad_maximum_fusion.5
  58.8 4.7 %collective-permute-start.7 = (bf16[4,128,128]{2,1,0:T(8,128)(2,1)}, bf16[4,128,128]{2,1,0:T(8,128)(2,1)}, u32[]{:S(2)}, u32[]{:S(2)}) collective-permute-start(bf16[4,128,128]{2,1,0:T(8,128)(2,1)} %pad_maximum_fusion.5), channel_id=1, source_target_pairs={{0,20},{1,21},{2,22},{3,23},{4,24},{5,25},{6,26},{7,27},{8,28},{9,... | collective-permute-start | bytes 393224 | tf_op jit(solution)/shard_map/ppermute | solution.py:250
  63.4 0.7 pad_maximum_fusion.4
  64.1 1.1 collective-permute-start.6
  65.2 0.7 pad_maximum_fusion.3
  65.9 5.0 %collective-permute-start.5 = (bf16[4,128,128]{2,1,0:T(8,128)(2,1)}, bf16[4,128,128]{2,1,0:T(8,128)(2,1)}, u32[]{:S(2)}, u32[]{:S(2)}) collective-permute-start(bf16[4,128,128]{2,1,0:T(8,128)(2,1)} %pad_maximum_fusion.3), channel_id=1, source_target_pairs={{0,12},{1,13},{2,14},{3,15},{4,16},{5,17},{6,18},{7,19},{8,20},{9,... | collective-permute-start | bytes 393224 | tf_op jit(solution)/shard_map/ppermute | solution.py:250
  70.9 0.7 pad_maximum_fusion.2
  71.6 0.7 pad_maximum_fusion.1
  72.2 26.9 %collective-permute-done.9.refs_8_ = bf16[4,128,128]{2,1,0:T(8,128)(2,1)S(1)} collective-permute-done((bf16[4,128,128]{2,1,0:T(8,128)(2,1)S(1)}, bf16[4,128,128]{2,1,0:T(8,128)(2,1)S(1)}, u32[]{:S(2)}, u32[]{:S(2)}) %collective-permute-start.9) | collective-permute-done | bytes 131104 | tf_op jit(solution)/shard_map/ppermute | solution.py:250
  99.7 5.8 %collective-permute-done.8.refs_7_ = bf16[4,128,128]{2,1,0:T(8,128)(2,1)S(1)} collective-permute-done((bf16[4,128,128]{2,1,0:T(8,128)(2,1)S(1)}, bf16[4,128,128]{2,1,0:T(8,128)(2,1)S(1)}, u32[]{:S(2)}, u32[]{:S(2)}) %collective-permute-start.8) | collective-permute-done | bytes 131104 | tf_op jit(solution)/shard_map/ppermute | solution.py:250
  105.6 0.6 copy-done
  106.2 2.1 %collective-permute-start.3 = (bf16[4,128,128]{2,1,0:T(8,128)(2,1)}, bf16[4,128,128]{2,1,0:T(8,128)(2,1)}, u32[]{:S(2)}, u32[]{:S(2)}) collective-permute-start(bf16[4,128,128]{2,1,0:T(8,128)(2,1)} %pad_maximum_fusion.1), channel_id=1, source_target_pairs={{0,4},{1,5},{2,6},{3,7},{4,8},{5,9},{6,10},{7,11},{8,12},{9,13},{1... | collective-permute-start | bytes 393224 | tf_op jit(solution)/shard_map/ppermute | solution.py:250
  108.4 0.9 unpack.1
  109.3 6.5 %collective-permute-done.7.refs_6_ = bf16[4,128,128]{2,1,0:T(8,128)(2,1)} collective-permute-done((bf16[4,128,128]{2,1,0:T(8,128)(2,1)}, bf16[4,128,128]{2,1,0:T(8,128)(2,1)}, u32[]{:S(2)}, u32[]{:S(2)}) %collective-permute-start.7) | collective-permute-done | bytes 131104 | tf_op jit(solution)/shard_map/ppermute | solution.py:250
  115.8 2.8 %collective-permute-start.10 = (bf16[16,2048]{1,0:T(8,128)(2,1)S(1)}, bf16[16,2048]{1,0:T(8,128)(2,1)S(1)}, u32[]{:S(2)}, u32[]{:S(2)}) collective-permute-start(bf16[16,2048]{1,0:T(8,128)(2,1)S(1)} %get-tuple-element.20), channel_id=1, source_target_pairs={{0,96},{32,0},{64,32},{96,64},{1,97},{33,1},{65,33},{97,65},{2,98}... | collective-permute-start | bytes 196616 | tf_op jit(solution)/shard_map/ppermute | solution.py:240
  118.6 5.2 %decode.1 = (bf16[16,32,2048]{2,1,0:T(8,128)(2,1)}, bf16[16,32,2048]{2,1,0:T(8,128)(2,1)}) custom-call(bf16[32,416,128]{2,1,0:T(8,128)(2,1)S(1)} %all-to-all-done.refs_0_, f32[32,32,128]{2,1,0:T(8,128)S(1)} %get-tuple-element.13.refs_1_.refs_9_), custom_call_target="tpu_custom_call" | custom-call | tf_op jit(solution)/shard_map/decode/pallas_call | solution.py:189
  123.8 0.8 collective-permute-start.11
  124.6 0.9 collective-permute-start.12
  125.5 3.9 %decode_rest.1 = (bf16[16,32,2048]{2,1,0:T(8,128)(2,1)}, bf16[16,32,2048]{2,1,0:T(8,128)(2,1)}) custom-call(s32[2]{0:T(128)S(1)} %copy-done.2, bf16[4,128,128]{2,1,0:T(8,128)(2,1)S(1)} %pad_maximum_fusion.refs_1_, bf16[4,128,128]{2,1,0:T(8,128)(2,1)} %collective-permute-done.3.refs_2_, ...), custom_call_target="tpu_custom_call", output_to_operand_aliasing={{0}: (10, {}), {1}: (11, {})} | custom-call | tf_op jit(solution)/shard_map/decode_rest/pallas_call | solution.py:217
  129.6 0.7 collective-permute-done.12
  130.3 0.7 dynamic-slice_bitcast_fusion
  (37 shorter events, 3.4 us)
Async XLA Ops:
  7.6 100.8 %all-to-all-start = ((bf16[32,416,128]{2,1,0:T(8,128)(2,1)}), bf16[32,416,128]{2,1,0:T(8,128)(2,1)S(1)}, u32[]{:S(2)}, u32[]{:S(2)}) async-start(bf16[32,416,128]{2,1,0:T(8,128)(2,1)} %encode.1), calls=%async_computation | async-start | bytes 6815744 | tf_op jit(solution)/shard_map/all_to_all | solution.py:258
  23.6 29.5 %collective-permute-start = (bf16[8,128,128]{2,1,0:T(8,128)(2,1)S(1)}, bf16[8,128,128]{2,1,0:T(8,128)(2,1)S(1)}, u32[]{:S(2)}, u32[]{:S(2)}) collective-permute-start(bf16[8,128,128]{2,1,0:T(8,128)(2,1)S(1)} %get-tuple-element.29), channel_id=1, source_target_pairs={{0,1},{1,2},{2,3},{3,0},{4,5},{5,6},{6,7},{7,4},{8,9},{9,10},{10,1... | collective-permute-start | bytes 786440 | tf_op jit(solution)/shard_map/ppermute | solution.py:250
  25.1 28.6 %collective-permute-start.1 = (bf16[8,128,128]{2,1,0:T(8,128)(2,1)S(1)}, bf16[8,128,128]{2,1,0:T(8,128)(2,1)S(1)}, u32[]{:S(2)}, u32[]{:S(2)}) collective-permute-start(bf16[8,128,128]{2,1,0:T(8,128)(2,1)S(1)} %get-tuple-element.31), channel_id=1, source_target_pairs={{0,2},{1,3},{2,0},{3,1},{4,6},{5,7},{6,4},{7,5},{8,10},{9,11},{10,... | collective-permute-start | bytes 786440 | tf_op jit(solution)/shard_map/ppermute | solution.py:250
  27.8 26.6 %collective-permute-start.2 = (bf16[8,128,128]{2,1,0:T(8,128)(2,1)S(1)}, bf16[8,128,128]{2,1,0:T(8,128)(2,1)S(1)}, u32[]{:S(2)}, u32[]{:S(2)}) collective-permute-start(bf16[8,128,128]{2,1,0:T(8,128)(2,1)S(1)} %get-tuple-element.30), channel_id=1, source_target_pairs={{0,3},{1,0},{2,1},{3,2},{4,7},{5,4},{6,5},{7,6},{8,11},{9,8},{10,9... | collective-permute-start | bytes 786440 | tf_op jit(solution)/shard_map/ppermute | solution.py:250
  55.0 44.2 %collective-permute-start.9 = (bf16[4,128,128]{2,1,0:T(8,128)(2,1)S(1)}, bf16[4,128,128]{2,1,0:T(8,128)(2,1)S(1)}, u32[]{:S(2)}, u32[]{:S(2)}) collective-permute-start(bf16[4,128,128]{2,1,0:T(8,128)(2,1)S(1)} %pad_maximum_fusion.7), channel_id=1, source_target_pairs={{0,28},{1,29},{2,30},{3,31},{4,0},{5,1},{6,2},{7,3},{8,4},{9,5},{1... | collective-permute-start | bytes 393224 | tf_op jit(solution)/shard_map/ppermute | solution.py:250
  56.8 48.8 %collective-permute-start.8 = (bf16[4,128,128]{2,1,0:T(8,128)(2,1)S(1)}, bf16[4,128,128]{2,1,0:T(8,128)(2,1)S(1)}, u32[]{:S(2)}, u32[]{:S(2)}) collective-permute-start(bf16[4,128,128]{2,1,0:T(8,128)(2,1)S(1)} %pad_maximum_fusion.6), channel_id=1, source_target_pairs={{0,24},{1,25},{2,26},{3,27},{4,28},{5,29},{6,30},{7,31},{8,0},{9,1... | collective-permute-start | bytes 393224 | tf_op jit(solution)/shard_map/ppermute | solution.py:250
  58.8 57.0 %collective-permute-start.7 = (bf16[4,128,128]{2,1,0:T(8,128)(2,1)}, bf16[4,128,128]{2,1,0:T(8,128)(2,1)}, u32[]{:S(2)}, u32[]{:S(2)}) collective-permute-start(bf16[4,128,128]{2,1,0:T(8,128)(2,1)} %pad_maximum_fusion.5), channel_id=1, source_target_pairs={{0,20},{1,21},{2,22},{3,23},{4,24},{5,25},{6,26},{7,27},{8,28},{9,... | collective-permute-start | bytes 393224 | tf_op jit(solution)/shard_map/ppermute | solution.py:250
  64.1 59.7 %collective-permute-start.6 = (bf16[4,128,128]{2,1,0:T(8,128)(2,1)}, bf16[4,128,128]{2,1,0:T(8,128)(2,1)}, u32[]{:S(2)}, u32[]{:S(2)}) collective-permute-start(bf16[4,128,128]{2,1,0:T(8,128)(2,1)} %pad_maximum_fusion.4), channel_id=1, source_target_pairs={{0,16},{1,17},{2,18},{3,19},{4,20},{5,21},{6,22},{7,23},{8,24},{9,... | collective-permute-start | bytes 393224 | tf_op jit(solution)/shard_map/ppermute | solution.py:250
  65.9 58.7 %collective-permute-start.5 = (bf16[4,128,128]{2,1,0:T(8,128)(2,1)}, bf16[4,128,128]{2,1,0:T(8,128)(2,1)}, u32[]{:S(2)}, u32[]{:S(2)}) collective-permute-start(bf16[4,128,128]{2,1,0:T(8,128)(2,1)} %pad_maximum_fusion.3), channel_id=1, source_target_pairs={{0,12},{1,13},{2,14},{3,15},{4,16},{5,17},{6,18},{7,19},{8,20},{9,... | collective-permute-start | bytes 393224 | tf_op jit(solution)/shard_map/ppermute | solution.py:250
  99.2 26.3 %collective-permute-start.4 = (bf16[4,128,128]{2,1,0:T(8,128)(2,1)}, bf16[4,128,128]{2,1,0:T(8,128)(2,1)}, u32[]{:S(2)}, u32[]{:S(2)}) collective-permute-start(bf16[4,128,128]{2,1,0:T(8,128)(2,1)} %pad_maximum_fusion.2), channel_id=1, source_target_pairs={{0,8},{1,9},{2,10},{3,11},{4,12},{5,13},{6,14},{7,15},{8,16},{9,17... | collective-permute-start | bytes 393224 | tf_op jit(solution)/shard_map/ppermute | solution.py:250
  105.6 0.7 copy-start
  106.2 19.3 %collective-permute-start.3 = (bf16[4,128,128]{2,1,0:T(8,128)(2,1)}, bf16[4,128,128]{2,1,0:T(8,128)(2,1)}, u32[]{:S(2)}, u32[]{:S(2)}) collective-permute-start(bf16[4,128,128]{2,1,0:T(8,128)(2,1)} %pad_maximum_fusion.1), channel_id=1, source_target_pairs={{0,4},{1,5},{2,6},{3,7},{4,8},{5,9},{6,10},{7,11},{8,12},{9,13},{1... | collective-permute-start | bytes 393224 | tf_op jit(solution)/shard_map/ppermute | solution.py:250
  108.3 17.2 %copy-start.2 = (s32[2]{0:T(128)S(1)}, s32[2]{0:T(128)}, u32[]{:S(2)}) copy-start(s32[2]{0:T(128)} %pad_add_fusion.refs_0_) | copy-start | bytes 28
  108.3 10.2 %copy-start.3 = (bf16[1,128,128]{2,1,0:T(8,128)(2,1)S(1)}, bf16[1,128,128]{2,1,0:T(8,128)(2,1)}, u32[]{:S(2)}) copy-start(bf16[1,128,128]{2,1,0:T(8,128)(2,1)} %get-tuple-element.28) | copy-start | bytes 98308
  108.3 10.2 %copy-start.4 = (bf16[1,128,128]{2,1,0:T(8,128)(2,1)S(1)}, bf16[1,128,128]{2,1,0:T(8,128)(2,1)}, u32[]{:S(2)}) copy-start(bf16[1,128,128]{2,1,0:T(8,128)(2,1)} %get-tuple-element.39) | copy-start | bytes 98308
  108.3 10.2 %copy-start.5 = (bf16[1,128,128]{2,1,0:T(8,128)(2,1)S(1)}, bf16[1,128,128]{2,1,0:T(8,128)(2,1)}, u32[]{:S(2)}) copy-start(bf16[1,128,128]{2,1,0:T(8,128)(2,1)} %get-tuple-element.47) | copy-start | bytes 98308
  108.3 10.2 %copy-start.6 = (bf16[1,128,128]{2,1,0:T(8,128)(2,1)S(1)}, bf16[1,128,128]{2,1,0:T(8,128)(2,1)}, u32[]{:S(2)}) copy-start(bf16[1,128,128]{2,1,0:T(8,128)(2,1)} %get-tuple-element.55) | copy-start | bytes 98308
  108.4 17.1 %copy-start.1 = (bf16[4,128,128]{2,1,0:T(8,128)(2,1)S(1)}, bf16[4,128,128]{2,1,0:T(8,128)(2,1)}, u32[]{:S(2)}) copy-start(bf16[4,128,128]{2,1,0:T(8,128)(2,1)} %copy-done) | copy-start | bytes 393220
  115.8 13.6 %collective-permute-start.10 = (bf16[16,2048]{1,0:T(8,128)(2,1)S(1)}, bf16[16,2048]{1,0:T(8,128)(2,1)S(1)}, u32[]{:S(2)}, u32[]{:S(2)}) collective-permute-start(bf16[16,2048]{1,0:T(8,128)(2,1)S(1)} %get-tuple-element.20), channel_id=1, source_target_pairs={{0,96},{32,0},{64,32},{96,64},{1,97},{33,1},{65,33},{97,65},{2,98}... | collective-permute-start | bytes 196616 | tf_op jit(solution)/shard_map/ppermute | solution.py:240
  123.8 5.8 %collective-permute-start.11 = (bf16[16,2048]{1,0:T(8,128)(2,1)S(1)}, bf16[16,2048]{1,0:T(8,128)(2,1)S(1)}, u32[]{:S(2)}, u32[]{:S(2)}) collective-permute-start(bf16[16,2048]{1,0:T(8,128)(2,1)S(1)} %get-tuple-element.20), channel_id=1, source_target_pairs={{0,64},{32,96},{64,0},{96,32},{1,65},{33,97},{65,1},{97,33},{2,66}... | collective-permute-start | bytes 196616 | tf_op jit(solution)/shard_map/ppermute | solution.py:240
  124.6 5.7 %collective-permute-start.12 = (bf16[16,2048]{1,0:T(8,128)(2,1)S(1)}, bf16[16,2048]{1,0:T(8,128)(2,1)S(1)}, u32[]{:S(2)}, u32[]{:S(2)}) collective-permute-start(bf16[16,2048]{1,0:T(8,128)(2,1)S(1)} %get-tuple-element.20), channel_id=1, source_target_pairs={{0,32},{32,64},{64,96},{96,0},{1,33},{33,65},{65,97},{97,1},{2,34}... | collective-permute-start | bytes 196616 | tf_op jit(solution)/shard_map/ppermute | solution.py:240

commit v4 on v3

v4 whole, which is shorter than its diff:
```python
import jax
import jax.numpy as jnp
from jax import lax
from jax.experimental import pallas as pl
from jax.experimental.pallas import tpu as pltpu
from jax.sharding import PartitionSpec as P

D_MODEL = 2048
LANES = 128
SPAN = 126.0
STEP = 250.0 / 26.0
LOW = 0.4 * 256
LN2 = 0.6931471805599453
GROUP = 4
DEEP, WIDE = 8, 4
ALL = pltpu.CompilerParams(vmem_limit_bytes=60 << 20)
SOME = pltpu.CompilerParams(vmem_limit_bytes=24 << 20)


def measured(total, top):
    high = total.astype(jnp.bfloat16).astype(jnp.float32)
    some = jnp.maximum(high, 1e-30)
    n = jnp.floor(jnp.log(jnp.maximum(some / jnp.maximum(top * 1.004, 1e-30), 0.9)) * (4 / LN2))
    f = 0.5 + (total - high) / some * LOW
    bound = high * jnp.exp2(n * -0.25)
    per = jnp.where(bound > 1e-30, SPAN / jnp.maximum(bound, 1e-30), 0.0)
    return high, jnp.exp2((n + 1 + f) * STEP - 125), per


def code_group(first, gates, ups, rows_ref, store):
    bands = gates.shape[2] // LANES
    total_ref, top_ref, per_ref = rows_ref.at[0], rows_ref.at[1], rows_ref.at[2]
    for i in range(GROUP):
        for k, array in enumerate((gates, ups)):
            for t in range(bands):
                lanes = slice(t * LANES, (t + 1) * LANES)
                size = jnp.abs(array[first + i, :, lanes])
                total_ref[2 * i + k : 2 * i + k + 1, lanes] = jnp.sum(size, axis=0, keepdims=True)
                top_ref[2 * i + k : 2 * i + k + 1, lanes] = jnp.max(size, axis=0, keepdims=True)
    high, low, per = measured(total_ref[...], top_ref[...])
    if store is not None:
        per_ref[...] = per
        for i in range(GROUP):
            for t in range(bands):
                lanes = slice(t * LANES, (t + 1) * LANES)
                both = [
                    jnp.exp2(array[first + i, :, lanes] * per_ref[2 * i + k : 2 * i + k + 1, lanes])
                    for k, array in enumerate((gates, ups))
                ]
                store(i, t, jnp.concatenate(both, axis=0).T.astype(jnp.bfloat16))
    return high, low


def encode_kernel(gate_ref, up_ref, router_from, gain_from, out_ref, *scratch, bands):
    gates, ups, codes, router_ref, gain_ref, stats_ref, rows_ref, into, small, out = scratch
    experts = gates.shape[0]
    sent = experts - GROUP

    def arrival(e):
        return (
            pltpu.make_async_copy(gate_ref.at[e], gates.at[e], into.at[0, e]),
            pltpu.make_async_copy(up_ref.at[e], ups.at[e], into.at[1, e]),
        )

    def leaving(first, count, k):
        rows = pl.ds(32 * first, count)
        return pltpu.make_async_copy(codes.at[:, rows], out_ref.at[:, rows], out.at[k])

    def group(g, code):
        first = g * GROUP
        for i in range(GROUP):
            for copy in arrival(first + i):
                copy.wait()

        def store(i, t, tile):
            for y in range(WIDE):
                codes[WIDE * t + y, pl.ds(pl.multiple_of((first + i) * 32, 32), 32)] = tile[32 * y : 32 * (y + 1)]

        high, low = code_group(first, gates, ups, rows_ref, store if code else None)
        stats_ref[pl.ds(pl.multiple_of(2 * first, 8), 2 * GROUP)] = high
        stats_ref[pl.ds(pl.multiple_of(2 * experts + 2 * first, 8), 2 * GROUP)] = low
        if code:
            leaving(first, 32 * GROUP, g).start()

    for e in range(experts):
        for copy in arrival(e):
            copy.start()
    parts = (
        pltpu.make_async_copy(router_from, router_ref, small.at[0]),
        pltpu.make_async_copy(gain_from, gain_ref, small.at[1]),
    )
    for copy in parts:
        copy.start()
    lax.fori_loop(0, sent // GROUP, lambda g, _: group(g, True), None)
    group(sent // GROUP, False)
    for copy in parts:
        copy.wait()
    router = (router_ref[...] * gain_ref[...]).astype(jnp.bfloat16).astype(jnp.float32)
    router = jnp.concatenate([router[:8], router[8:]], axis=1).astype(jnp.bfloat16)
    for t in range(bands):
        tile = stats_ref[:, t * LANES : (t + 1) * LANES].T
        for y in range(WIDE):
            part = tile[32 * y : 32 * (y + 1), :64]
            codes[WIDE * t + y, 32 * sent : 32 * sent + 16] = jnp.concatenate([part[:16], part[16:]], axis=1).astype(jnp.bfloat16)
            codes[WIDE * t + y, 32 * sent + 16 :] = router
    leaving(sent, EXTRA, sent // GROUP).start()
    for k in range(sent // GROUP):
        leaving(k * GROUP, 32 * GROUP, k).wait()
    leaving(sent, EXTRA, sent // GROUP).wait()


EXTRA = 24


def encode(w_gate, w_up, router, gain):
    experts, _, columns = w_gate.shape
    sent = experts - GROUP
    shape = (32, 32 * sent + EXTRA, LANES)
    anywhere = pl.BlockSpec(memory_space=pl.ANY)
    return pl.pallas_call(
        lambda *refs: encode_kernel(*refs, bands=columns // LANES),
        name="encode",
        in_specs=[anywhere] * 4,
        out_specs=anywhere,
        out_shape=jax.ShapeDtypeStruct(shape, jnp.bfloat16),
        scratch_shapes=[
            pltpu.VMEM(w_gate.shape, jnp.float32),
            pltpu.VMEM(w_up.shape, jnp.float32),
            pltpu.VMEM(shape, jnp.bfloat16),
            pltpu.VMEM(router.shape, jnp.float32),
            pltpu.VMEM(gain.shape, jnp.float32),
            pltpu.VMEM((LANES, columns), jnp.float32),
            pltpu.VMEM((3, 2 * GROUP, columns), jnp.float32),
            pltpu.SemaphoreType.DMA((2, experts)),
            pltpu.SemaphoreType.DMA((2,)),
            pltpu.SemaphoreType.DMA((sent // GROUP + 1,)),
        ],
        compiler_params=ALL,
    )(w_gate, w_up, router, gain)


def encode_rest_kernel(at_ref, gate_ref, up_ref, out_ref, rows_ref):
    z, y = at_ref[0], at_ref[1]

    def store(i, t, tile):
        for k in range(WIDE):
            to = (k - y) % WIDE * DEEP + (t - z) % DEEP
            out_ref[to, 32 * i : 32 * (i + 1)] = tile[32 * k : 32 * (k + 1)]

    code_group(0, gate_ref, up_ref, rows_ref, store)


def encode_rest(at, w_gate, w_up):
    experts, rows, columns = w_gate.shape
    return pl.pallas_call(
        encode_rest_kernel,
        name="encode_rest",
        grid_spec=pltpu.PrefetchScalarGridSpec(
            num_scalar_prefetch=1,
            grid=(1,),
            in_specs=[pl.BlockSpec((GROUP, rows, columns), lambda _, at: (experts // GROUP - 1, 0, 0))] * 2,
            out_specs=pl.BlockSpec((32, 32 * GROUP, LANES), lambda _, at: (0, 0, 0)),
            scratch_shapes=[pltpu.VMEM((3, 2 * GROUP, columns), jnp.float32)],
        ),
        out_shape=jax.ShapeDtypeStruct((32, 32 * GROUP, LANES), jnp.bfloat16),
        compiler_params=ALL,
    )(at, w_gate, w_up)


def unpack_kernel(extra_ref, factor_ref, scale_ref, router_ref, *, experts):
    extra = extra_ref[...].astype(jnp.float32)
    lane = lax.broadcasted_iota(jnp.int32, (32, LANES), 1)
    scale = jnp.zeros((32, LANES), jnp.float32)
    for s in range(32):
        high = jnp.concatenate([extra[s, :16], pltpu.roll(extra[s, :16], 64, 1)], axis=0)
        low = pltpu.roll(high, LANES - 2 * experts, 1)
        at = (jnp.log(jnp.maximum(low, 1e-38)) * (1 / LN2) + 125) * (1 / STEP)
        n = jnp.floor(at)
        scale += high * (1 + (at - n - 0.5) * (1 / LOW))
        factor_ref[s] = high * jnp.exp2((n - 1) * -0.25) * (1.0 / (SPAN * LN2))
    scale = scale / D_MODEL
    for s in range(32):
        factor_ref[s] = jnp.where(lane < 2 * experts, factor_ref[s] / scale, 0.0)
    scale_ref[...] = jnp.concatenate([scale] * 4, axis=0).T[: 2 * experts, :32]
    left = lax.broadcasted_iota(jnp.int32, (8, LANES), 1) < 64
    for p in range(16):
        one, two = extra[2 * p, 16:], extra[2 * p + 1, 16:]
        both = [jnp.where(left, one, pltpu.roll(two, 64, 1)), jnp.where(left, pltpu.roll(one, 64, 1), two)]
        router_ref[:, p * LANES : (p + 1) * LANES] = jnp.concatenate(both, axis=0).astype(jnp.bfloat16)


def unpack(got, experts):
    whole = lambda shape: pl.BlockSpec(shape, lambda _: (0,) * len(shape))
    return pl.pallas_call(
        lambda *refs: unpack_kernel(*refs, experts=experts),
        name="unpack",
        grid=(1,),
        in_specs=[pl.BlockSpec((32, EXTRA, LANES), lambda _: (0, 32 * (experts - GROUP) // EXTRA, 0))],
        out_specs=[whole((32, 32, LANES)), whole((2 * experts, 32)), whole((16, D_MODEL))],
        out_shape=[
            jax.ShapeDtypeStruct((32, 32, LANES), jnp.float32),
            jax.ShapeDtypeStruct((2 * experts, 32), jnp.float32),
            jax.ShapeDtypeStruct((16, D_MODEL), jnp.bfloat16),
        ],
        compiler_params=SOME,
    )(got)


def decoded(read, factor_ref, gate_ref, up_ref, value_ref, first):
    to = lax.broadcasted_iota(jnp.int32, (2 * LANES, 2 * LANES), 1)
    of = lax.broadcasted_iota(jnp.int32, (2 * LANES, 2 * LANES), 0)
    move = of == to % 64 + to // 64 % 2 * LANES + to // LANES * 64
    move = jnp.where(move, 1.0, 0.0).astype(jnp.bfloat16)

    def one(i, _):
        row = pl.multiple_of(i * 32, 32)
        e = first + i
        which = 2 * e + lax.broadcasted_iota(jnp.int32, (32, LANES), 1) // 64
        for s in range(32):
            factor = jnp.take_along_axis(factor_ref[s], which, axis=1)
            value = (jnp.log(read(s, row).astype(jnp.float32)) * factor).astype(jnp.bfloat16)
            value_ref[i, s // 2 * 32 : s // 2 * 32 + 32, s % 2 * LANES : (s % 2 + 1) * LANES] = value
        both = jnp.dot(value_ref[i], move, preferred_element_type=jnp.float32).astype(jnp.bfloat16)
        for p in range(16):
            gate_ref[i, :, p * LANES : (p + 1) * LANES] = both[p * 32 : (p + 1) * 32, :LANES]
            up_ref[i, :, p * LANES : (p + 1) * LANES] = both[p * 32 : (p + 1) * 32, LANES:]

    lax.fori_loop(0, GROUP, one, None, unroll=2)


def decode_kernel(got_ref, factor_ref, gate_ref, up_ref, value_ref):
    read = lambda s, row: got_ref[s, pl.ds(row, 32)]
    decoded(read, factor_ref, gate_ref, up_ref, value_ref, pl.program_id(0) * GROUP)


def decode(got, factor, experts):
    out = jax.ShapeDtypeStruct((experts, 32, D_MODEL), jnp.bfloat16)
    return pl.pallas_call(
        lambda *refs: decode_kernel(*refs),
        name="decode",
        grid=(experts // GROUP - 1,),
        in_specs=[
            pl.BlockSpec((32, 32 * GROUP, LANES), lambda g: (0, g, 0)),
            pl.BlockSpec((32, 32, LANES), lambda g: (0, 0, 0)),
        ],
        out_specs=[pl.BlockSpec((GROUP, 32, D_MODEL), lambda g: (g, 0, 0))] * 2,
        out_shape=[out, out],
        scratch_shapes=[pltpu.VMEM((GROUP, 512, 2 * LANES), jnp.bfloat16)],
        compiler_params=SOME,
    )(got, factor)


def decode_rest_kernel(at_ref, *refs, experts):
    parts, (factor_ref, _, _, gate_ref, up_ref, got_ref, value_ref) = refs[:DEEP], refs[DEEP:]
    z, y = at_ref[0], at_ref[1]
    for k, part in enumerate(parts):
        for j in range(WIDE):
            got_ref[(z - k) % DEEP * WIDE + (y - j) % WIDE] = part[j]
    read = lambda s, row: got_ref[s, pl.ds(row, 32)]
    decoded(read, factor_ref, gate_ref, up_ref, value_ref, experts - GROUP)


def decode_rest(at, parts, factor, gate, up):
    experts = gate.shape[0]
    last = experts // GROUP - 1
    return pl.pallas_call(
        lambda *refs: decode_rest_kernel(*refs, experts=experts),
        name="decode_rest",
        grid_spec=pltpu.PrefetchScalarGridSpec(
            num_scalar_prefetch=1,
            grid=(1,),
            in_specs=[pl.BlockSpec(parts[0].shape, lambda _, at: (0, 0, 0))] * DEEP
            + [pl.BlockSpec((32, 32, LANES), lambda _, at: (0, 0, 0))]
            + [pl.BlockSpec(memory_space=pl.ANY)] * 2,
            out_specs=[pl.BlockSpec((GROUP, 32, D_MODEL), lambda _, at: (last, 0, 0))] * 2,
            scratch_shapes=[
                pltpu.VMEM((32, 32 * GROUP, LANES), jnp.bfloat16),
                pltpu.VMEM((GROUP, 512, 2 * LANES), jnp.bfloat16),
            ],
        ),
        out_shape=[jax.ShapeDtypeStruct(gate.shape, gate.dtype)] * 2,
        input_output_aliases={DEEP + 2: 0, DEEP + 3: 1},
        compiler_params=SOME,
    )(at, *parts, factor, gate, up)


def joined(array, axis):
    count, me = lax.axis_size(axis), lax.axis_index(axis)
    near = [array] + [lax.ppermute(array, axis, [(s, (s + k) % count) for s in range(count)]) for k in range(1, count)]
    ring = jnp.concatenate((near[::-1] * 2)[: 2 * count - 1])
    return lax.dynamic_slice_in_dim(ring, (count - 1 - me) * len(array), count * len(array))


def offset(array, deep, wide):
    pairs = []
    for s in range(DEEP * WIDE):
        z, y = divmod(s, WIDE)
        pairs.append((s, (z + deep) % DEEP * WIDE + (y + wide) % WIDE))
    return lax.ppermute(array, "zero", pairs)


def local(w_gate, w_up, router_weight, router_gain):
    experts = w_gate.shape[0]
    me = lax.axis_index("zero")
    at = jnp.stack([me // WIDE, me % WIDE]).astype(jnp.int32)
    sent = encode(w_gate, w_up, router_weight.T, router_gain[None])
    got = lax.all_to_all(sent, "zero", 0, 0, tiled=True)
    rest = encode_rest(at, w_gate, w_up)
    rows = [rest[:DEEP]]
    for k in range(1, WIDE):
        rows.append(offset(rest[DEEP * k : DEEP * (k + 1)], 0, k))
    parts = [jnp.stack([row[k] for row in rows]) for k in range(DEEP)]
    for k in range(1, DEEP):
        parts[k] = offset(parts[k], k, 0)
    factor, scale, router = unpack(got, experts)
    gate, up = decode(got, factor, experts)
    router = joined(router, "bank").T
    at, router, scale = lax.optimization_barrier((at, router, scale.reshape(experts, 2, 32).swapaxes(0, 1)))
    gate, up = decode_rest(at, parts, factor, gate, up)
    return jnp.swapaxes(gate, 1, 2), jnp.swapaxes(up, 1, 2), scale[0], scale[1], router


def solution(mesh):
    placed = (
        P(("trial", "bank"), "zero", None),
        P(("trial", "bank"), "zero", None),
        P(("trial", "zero"), "bank"),
        P(("trial", "zero")),
    )
    return jax.shard_map(
        local,
        mesh=mesh,
        in_specs=placed,
        out_specs=(
            P(("trial", "bank"), None, "zero"),
            P(("trial", "bank"), None, "zero"),
            P(("trial", "bank"), "zero"),
            P(("trial", "bank"), "zero"),
            P("trial", None),
        ),
        check_vma=False,
    )
```

time: 131 us -> 136 us (1.038)
  the two profiles are of different devices: /device:TPU:96 before, /device:TPU:56 now
where the time goes in v4:
time: 136 us; the launch traced here: 135 us
  waiting for transfers between devices  65.7 us (48%)
  starting transfers between devices  31.2 us (23%)
  Pallas kernels  18.7 us (14%)
  local copies, waits for them, and re-layouts  9.49 us (7%)
  other arithmetic  9.1 us (7%)
    ppermute x10, waiting for transfers between devices, offset(): return lax.ppermute(array, 'zero', pairs)  31.1 us
    all_to_all x1, waiting for transfers between devices, local(): got = lax.all_to_all(sent, 'zero', 0, 0, tiled=True)  24.2 us
    ppermute x10, starting transfers between devices, offset(): return lax.ppermute(array, 'zero', pairs)  16.5 us
    all_to_all x1, starting transfers between devices, local(): got = lax.all_to_all(sent, 'zero', 0, 0, tiled=True)  11 us
    ppermute x3, waiting for transfers between devices, joined(): lax.ppermute(array, axis, [(s, (s + k) % count) for s in range(count)])  10.4 us
    another operation x8, other arithmetic, local(): parts = [jnp.stack([row[k] for row in rows]) for k in range(DEEP)]  8.49 us
    slice x4, local copies, waits for them, and re-layouts, local(): parts = [jnp.stack([row[k] for row in rows]) for k in range(DEEP)]  6.07 us
    pallas_call x1, Pallas kernels, encode(): pl.pallas_call(lambda *refs: encode_kernel(*refs, bands=columns // LANES)...  5.31 us
  transfers between devices with their start and end apart: 14, of which 9 were waited for; matrix products, arithmetic and copies ran while one was open for 14% of the time, Pallas kernels for 7%

profile of v4, /device:TPU:56, one launch (start us, length us, event | category | flops | bytes accessed | tf_op | source)
XLA Modules:
  0.0 134.9 jit_solution(4998486280445068428)
XLA Ops:
  0.6 5.3 %encode.1 = bf16[32,408,128]{2,1,0:T(8,128)(2,1)} custom-call(f32[16,64,1024]{2,1,0:T(8,128)} %gate_ref.1, f32[16,64,1024]{2,1,0:T(8,128)} %up_ref.1, f32[16,64]{1,0:T(8,128)} %bitcast.20, f32[1,64]{1,0:T(1,128)} %bitcast.21), custom_call_target="tpu_custom_call" | custom-call | tf_op jit(solution)/shard_map/encode/pallas_call | solution.py:120
  6.0 11.0 %all-to-all-start = ((bf16[32,408,128]{2,1,0:T(8,128)(2,1)}), bf16[32,408,128]{2,1,0:T(8,128)(2,1)S(1)}, u32[]{:S(2)}, u32[]{:S(2)}) async-start(bf16[32,408,128]{2,1,0:T(8,128)(2,1)} %encode.1), calls=%async_computation | async-start | bytes 6684672 | tf_op jit(solution)/shard_map/all_to_all | solution.py:307
  17.6 3.9 %encode_rest.1 = bf16[32,128,128]{2,1,0:T(8,128)(2,1)} custom-call(s32[2]{0:T(128)} %pad_add_fusion.at_ref.refs_0_, f32[16,64,1024]{2,1,0:T(8,128)} %gate_ref.1, f32[16,64,1024]{2,1,0:T(8,128)} %up_ref.1), custom_call_target="tpu_custom_call" | custom-call | tf_op jit(solution)/shard_map/encode_rest/pallas_call | solution.py:155
  21.5 2.0 %fusion.1 = (bf16[8,128,128]{2,1,0:T(8,128)(2,1)}, bf16[8,128,128]{2,1,0:T(8,128)(2,1)}, bf16[8,128,128]{2,1,0:T(8,128)(2,1)}) fusion(bf16[32,128,128]{2,1,0:T(8,128)(2,1)} %encode_rest.1), kind=kLoop, calls=%fused_computation.21 | loop fusion | bytes 1572864 | tf_op jit(solution)/shard_map/slice | solution.py:311
  24.1 1.5 %collective-permute-start.5 = (bf16[8,128,128]{2,1,0:T(8,128)(2,1)}, bf16[8,128,128]{2,1,0:T(8,128)(2,1)}, u32[]{:S(2)}, u32[]{:S(2)}) collective-permute-start(bf16[8,128,128]{2,1,0:T(8,128)(2,1)} %get-tuple-element.34), channel_id=1, source_target_pairs={{0,3},{1,0},{2,1},{3,2},{4,7},{5,4},{6,5},{7,6},{8,11},{9,8},{10,9... | collective-permute-start | bytes 786440 | tf_op jit(solution)/shard_map/ppermute | solution.py:299
  25.6 1.5 %collective-permute-start.4 = (bf16[8,128,128]{2,1,0:T(8,128)(2,1)}, bf16[8,128,128]{2,1,0:T(8,128)(2,1)}, u32[]{:S(2)}, u32[]{:S(2)}) collective-permute-start(bf16[8,128,128]{2,1,0:T(8,128)(2,1)} %get-tuple-element.35), channel_id=1, source_target_pairs={{0,2},{1,3},{2,0},{3,1},{4,6},{5,7},{6,4},{7,5},{8,10},{9,11},{10,... | collective-permute-start | bytes 786440 | tf_op jit(solution)/shard_map/ppermute | solution.py:299
  27.0 1.6 %fusion = (bf16[1,128,128]{2,1,0:T(8,128)(2,1)}, bf16[1,128,128]{2,1,0:T(8,128)(2,1)}, bf16[1,128,128]{2,1,0:T(8,128)(2,1)S(1)}, bf16[1,128,128]{2,1,0:T(8,128)(...) fusion(bf16[32,128,128]{2,1,0:T(8,128)(2,1)} %encode_rest.1), kind=kLoop, calls=%fused_computation.20 | loop fusion | bytes 524288 | tf_op jit(solution)/shard_map/slice | solution.py:312
  28.6 8.9 %collective-permute-done.3 = bf16[8,128,128]{2,1,0:T(8,128)(2,1)} collective-permute-done((bf16[8,128,128]{2,1,0:T(8,128)(2,1)}, bf16[8,128,128]{2,1,0:T(8,128)(2,1)}, u32[]{:S(2)}, u32[]{:S(2)}) %collective-permute-start.3) | collective-permute-done | bytes 262176 | tf_op jit(solution)/shard_map/ppermute | solution.py:299
  37.5 1.5 %fusion.2 = (bf16[1,128,128]{2,1,0:T(8,128)(2,1)S(1)}, bf16[1,128,128]{2,1,0:T(8,128)(2,1)S(1)}, bf16[1,128,128]{2,1,0:T(8,128)(2,1)S(1)}, bf16[1,128,128]{2,1,0...) fusion(bf16[8,128,128]{2,1,0:T(8,128)(2,1)} %collective-permute, ...), kind=kLoop, calls=%fused_computation.22 | loop fusion | bytes 524288 | tf_op jit(solution)/shard_map/slice | solution.py:312
  39.0 3.6 %collective-permute-done.5 = bf16[8,128,128]{2,1,0:T(8,128)(2,1)} collective-permute-done((bf16[8,128,128]{2,1,0:T(8,128)(2,1)}, bf16[8,128,128]{2,1,0:T(8,128)(2,1)}, u32[]{:S(2)}, u32[]{:S(2)}) %collective-permute-start.5) | collective-permute-done | bytes 262176 | tf_op jit(solution)/shard_map/ppermute | solution.py:299
  42.6 1.5 %fusion.4 = (bf16[1,128,128]{2,1,0:T(8,128)(2,1)S(1)}, bf16[1,128,128]{2,1,0:T(8,128)(2,1)S(1)}, bf16[1,128,128]{2,1,0:T(8,128)(2,1)S(1)}, bf16[1,128,128]{2,1,0...) fusion(bf16[8,128,128]{2,1,0:T(8,128)(2,1)} %collective-permute, ...), kind=kLoop, calls=%fused_computation.24 | loop fusion | bytes 524288 | tf_op jit(solution)/shard_map/slice | solution.py:312
  44.1 6.9 %collective-permute-done.4 = bf16[8,128,128]{2,1,0:T(8,128)(2,1)} collective-permute-done((bf16[8,128,128]{2,1,0:T(8,128)(2,1)}, bf16[8,128,128]{2,1,0:T(8,128)(2,1)}, u32[]{:S(2)}, u32[]{:S(2)}) %collective-permute-start.4) | collective-permute-done | bytes 262176 | tf_op jit(solution)/shard_map/ppermute | solution.py:299
  51.0 1.5 %fusion.3 = (bf16[1,128,128]{2,1,0:T(8,128)(2,1)S(1)}, bf16[1,128,128]{2,1,0:T(8,128)(2,1)S(1)}, bf16[1,128,128]{2,1,0:T(8,128)(2,1)S(1)}, bf16[1,128,128]{2,1,0...) fusion(bf16[8,128,128]{2,1,0:T(8,128)(2,1)} %collective-permute, ...), kind=kLoop, calls=%fused_computation.23 | loop fusion | bytes 524288 | tf_op jit(solution)/shard_map/slice | solution.py:312
  53.1 4.2 %collective-permute-start.6 = (bf16[4,128,128]{2,1,0:T(8,128)(2,1)}, bf16[4,128,128]{2,1,0:T(8,128)(2,1)S(1)}, u32[]{:S(2)}, u32[]{:S(2)}) collective-permute-start(bf16[4,128,128]{2,1,0:T(8,128)(2,1)} %pad_maximum_fusion.1), channel_id=1, source_target_pairs={{0,4},{1,5},{2,6},{3,7},{4,8},{5,9},{6,10},{7,11},{8,12},{9,13},{1... | collective-permute-start | bytes 393224 | tf_op jit(solution)/shard_map/ppermute | solution.py:299
  57.3 1.4 %pad_maximum_fusion.2 = bf16[4,128,128]{2,1,0:T(8,128)(2,1)} fusion(bf16[1,128,128]{2,1,0:T(8,128)(2,1)S(1)} %get-tuple-element.57, bf16[1,128,128]{2,1,0:T(8,128)(2,1)S(1)} %get-tuple-element.49, bf16[1,128,128]{2,1,0:T(8,128)(2,1)S(1)} %get-tuple-element.41, bf16[1,128,128]{2,1,0:T(8,128)(2,1)} %get-tuple-element.30), kind=kLoop, calls=%fused_computation.3 | loop fusion | flops 196608 | bytes 262144 | tf_op jit(solution)/shard_map/stack | solution.py:312
  58.7 3.7 %collective-permute-start.7 = (bf16[4,128,128]{2,1,0:T(8,128)(2,1)}, bf16[4,128,128]{2,1,0:T(8,128)(2,1)}, u32[]{:S(2)}, u32[]{:S(2)}) collective-permute-start(bf16[4,128,128]{2,1,0:T(8,128)(2,1)} %pad_maximum_fusion.2), channel_id=1, source_target_pairs={{0,8},{1,9},{2,10},{3,11},{4,12},{5,13},{6,14},{7,15},{8,16},{9,17... | collective-permute-start | bytes 393224 | tf_op jit(solution)/shard_map/ppermute | solution.py:299
  62.5 1.4 %pad_maximum_fusion.3 = bf16[4,128,128]{2,1,0:T(8,128)(2,1)} fusion(bf16[1,128,128]{2,1,0:T(8,128)(2,1)S(1)} %get-tuple-element.56, bf16[1,128,128]{2,1,0:T(8,128)(2,1)S(1)} %get-tuple-element.48, bf16[1,128,128]{2,1,0:T(8,128)(2,1)S(1)} %get-tuple-element.40, bf16[1,128,128]{2,1,0:T(8,128)(2,1)} %get-tuple-element.29), kind=kLoop, calls=%fused_computation.4 | loop fusion | flops 196608 | bytes 262144 | tf_op jit(solution)/shard_map/stack | solution.py:312
  64.4 1.4 %pad_maximum_fusion.4 = bf16[4,128,128]{2,1,0:T(8,128)(2,1)} fusion(bf16[1,128,128]{2,1,0:T(8,128)(2,1)S(1)} %get-tuple-element.55, bf16[1,128,128]{2,1,0:T(8,128)(2,1)S(1)} %get-tuple-element.47, bf16[1,128,128]{2,1,0:T(8,128)(2,1)S(1)} %get-tuple-element.39, bf16[1,128,128]{2,1,0:T(8,128)(2,1)} %get-tuple-element.28), kind=kLoop, calls=%fused_computation.5 | loop fusion | flops 196608 | bytes 262144 | tf_op jit(solution)/shard_map/stack | solution.py:312
  65.9 2.3 %collective-permute-start.9 = (bf16[4,128,128]{2,1,0:T(8,128)(2,1)}, bf16[4,128,128]{2,1,0:T(8,128)(2,1)}, u32[]{:S(2)}, u32[]{:S(2)}) collective-permute-start(bf16[4,128,128]{2,1,0:T(8,128)(2,1)} %pad_maximum_fusion.4), channel_id=1, source_target_pairs={{0,16},{1,17},{2,18},{3,19},{4,20},{5,21},{6,22},{7,23},{8,24},{9,... | collective-permute-start | bytes 393224 | tf_op jit(solution)/shard_map/ppermute | solution.py:299
  68.1 1.4 %pad_maximum_fusion.7 = bf16[4,128,128]{2,1,0:T(8,128)(2,1)} fusion(bf16[1,128,128]{2,1,0:T(8,128)(2,1)S(1)} %get-tuple-element.52, bf16[1,128,128]{2,1,0:T(8,128)(2,1)S(1)} %get-tuple-element.44, bf16[1,128,128]{2,1,0:T(8,128)(2,1)S(1)} %get-tuple-element.36, bf16[1,128,128]{2,1,0:T(8,128)(2,1)} %get-tuple-element.25), kind=kLoop, calls=%fused_computation.8 | loop fusion | flops 196608 | bytes 262144 | tf_op jit(solution)/shard_map/stack | solution.py:312
  69.6 1.4 %pad_maximum_fusion.6 = bf16[4,128,128]{2,1,0:T(8,128)(2,1)} fusion(bf16[1,128,128]{2,1,0:T(8,128)(2,1)S(1)} %get-tuple-element.53, bf16[1,128,128]{2,1,0:T(8,128)(2,1)S(1)} %get-tuple-element.45, bf16[1,128,128]{2,1,0:T(8,128)(2,1)S(1)} %get-tuple-element.37, bf16[1,128,128]{2,1,0:T(8,128)(2,1)} %get-tuple-element.26), kind=kLoop, calls=%fused_computation.7 | loop fusion | flops 196608 | bytes 262144 | tf_op jit(solution)/shard_map/stack | solution.py:312
  71.7 24.2 %all-to-all-done.refs_0_ = bf16[32,408,128]{2,1,0:T(8,128)(2,1)S(1)} async-done(((bf16[32,408,128]{2,1,0:T(8,128)(2,1)}), bf16[32,408,128]{2,1,0:T(8,128)(2,1)S(1)}, u32[]{:S(2)}, u32[]{:S(2)}) %all-to-all-start) | async-done | bytes 3342368 | tf_op jit(solution)/shard_map/all_to_all | solution.py:307
  96.4 2.8 %collective-permute-start = (bf16[16,2048]{1,0:T(8,128)(2,1)S(1)}, bf16[16,2048]{1,0:T(8,128)(2,1)S(1)}, u32[]{:S(2)}, u32[]{:S(2)}) collective-permute-start(bf16[16,2048]{1,0:T(8,128)(2,1)S(1)} %get-tuple-element.15), channel_id=1, source_target_pairs={{0,96},{32,0},{64,32},{96,64},{1,97},{33,1},{65,33},{97,65},{2,98}... | collective-permute-start | bytes 196616 | tf_op jit(solution)/shard_map/ppermute | solution.py:289
  99.3 5.2 %decode.1 = (bf16[16,32,2048]{2,1,0:T(8,128)(2,1)}, bf16[16,32,2048]{2,1,0:T(8,128)(2,1)}) custom-call(bf16[32,408,128]{2,1,0:T(8,128)(2,1)S(1)} %all-to-all-done.refs_0_, f32[32,32,128]{2,1,0:T(8,128)S(1)} %get-tuple-element.18.refs_1_.refs_9_), custom_call_target="tpu_custom_call" | custom-call | tf_op jit(solution)/shard_map/decode/pallas_call | solution.py:238
  104.5 0.8 collective-permute-start.1
  105.3 5.0 %collective-permute-done.1 = bf16[16,2048]{1,0:T(8,128)(2,1)S(1)} collective-permute-done((bf16[16,2048]{1,0:T(8,128)(2,1)S(1)}, bf16[16,2048]{1,0:T(8,128)(2,1)S(1)}, u32[]{:S(2)}, u32[]{:S(2)}) %collective-permute-start.1) | collective-permute-done | bytes 65568 | tf_op jit(solution)/shard_map/ppermute | solution.py:289
  110.3 5.5 %collective-permute-done.2 = bf16[16,2048]{1,0:T(8,128)(2,1)S(1)} collective-permute-done((bf16[16,2048]{1,0:T(8,128)(2,1)S(1)}, bf16[16,2048]{1,0:T(8,128)(2,1)S(1)}, u32[]{:S(2)}, u32[]{:S(2)}) %collective-permute-start.2) | collective-permute-done | bytes 65568 | tf_op jit(solution)/shard_map/ppermute | solution.py:289
  115.8 0.7 dynamic-slice_bitcast_fusion
  117.3 1.6 %collective-permute-start.12 = (bf16[4,128,128]{2,1,0:T(8,128)(2,1)S(1)}, bf16[4,128,128]{2,1,0:T(8,128)(2,1)S(1)}, u32[]{:S(2)}, u32[]{:S(2)}) collective-permute-start(bf16[4,128,128]{2,1,0:T(8,128)(2,1)S(1)} %copy-done.1), channel_id=1, source_target_pairs={{0,28},{1,29},{2,30},{3,31},{4,0},{5,1},{6,2},{7,3},{8,4},{9,5},{1... | collective-permute-start | bytes 393224 | tf_op jit(solution)/shard_map/ppermute | solution.py:299
  119.5 8.2 %collective-permute-done.10.refs_6_ = bf16[4,128,128]{2,1,0:T(8,128)(2,1)S(1)} collective-permute-done((bf16[4,128,128]{2,1,0:T(8,128)(2,1)S(1)}, bf16[4,128,128]{2,1,0:T(8,128)(2,1)S(1)}, u32[]{:S(2)}, u32[]{:S(2)}) %collective-permute-start.10) | collective-permute-done | bytes 131104 | tf_op jit(solution)/shard_map/ppermute | solution.py:299
  127.7 3.4 %collective-permute-done.11.refs_7_ = bf16[4,128,128]{2,1,0:T(8,128)(2,1)S(1)} collective-permute-done((bf16[4,128,128]{2,1,0:T(8,128)(2,1)S(1)}, bf16[4,128,128]{2,1,0:T(8,128)(2,1)S(1)}, u32[]{:S(2)}, u32[]{:S(2)}) %collective-permute-start.11) | collective-permute-done | bytes 131104 | tf_op jit(solution)/shard_map/ppermute | solution.py:299
  131.2 3.8 %decode_rest.1 = (bf16[16,32,2048]{2,1,0:T(8,128)(2,1)}, bf16[16,32,2048]{2,1,0:T(8,128)(2,1)}) custom-call(s32[2]{0:T(128)S(1)} %copy-done, bf16[4,128,128]{2,1,0:T(8,128)(2,1)S(1)} %pad_maximum_fusion.refs_1_, bf16[4,128,128]{2,1,0:T(8,128)(2,1)S(1)} %collective-permute-done.6.refs_2_, ...), custom_call_target="tpu_custom_call", output_to_operand_aliasing={{0}: (10, {}), {1}: (11, {})} | custom-call | tf_op jit(solution)/shard_map/decode_rest/pallas_call | solution.py:266
  (39 shorter events, 5.1 us)
Async XLA Ops:
  6.0 89.9 %all-to-all-start = ((bf16[32,408,128]{2,1,0:T(8,128)(2,1)}), bf16[32,408,128]{2,1,0:T(8,128)(2,1)S(1)}, u32[]{:S(2)}, u32[]{:S(2)}) async-start(bf16[32,408,128]{2,1,0:T(8,128)(2,1)} %encode.1), calls=%async_computation | async-start | bytes 6684672 | tf_op jit(solution)/shard_map/all_to_all | solution.py:307
  23.5 14.0 %collective-permute-start.3 = (bf16[8,128,128]{2,1,0:T(8,128)(2,1)}, bf16[8,128,128]{2,1,0:T(8,128)(2,1)}, u32[]{:S(2)}, u32[]{:S(2)}) collective-permute-start(bf16[8,128,128]{2,1,0:T(8,128)(2,1)} %get-tuple-element.33), channel_id=1, source_target_pairs={{0,1},{1,2},{2,3},{3,0},{4,5},{5,6},{6,7},{7,4},{8,9},{9,10},{10,1... | collective-permute-start | bytes 786440 | tf_op jit(solution)/shard_map/ppermute | solution.py:299
  24.1 18.5 %collective-permute-start.5 = (bf16[8,128,128]{2,1,0:T(8,128)(2,1)}, bf16[8,128,128]{2,1,0:T(8,128)(2,1)}, u32[]{:S(2)}, u32[]{:S(2)}) collective-permute-start(bf16[8,128,128]{2,1,0:T(8,128)(2,1)} %get-tuple-element.34), channel_id=1, source_target_pairs={{0,3},{1,0},{2,1},{3,2},{4,7},{5,4},{6,5},{7,6},{8,11},{9,8},{10,9... | collective-permute-start | bytes 786440 | tf_op jit(solution)/shard_map/ppermute | solution.py:299
  25.6 25.4 %collective-permute-start.4 = (bf16[8,128,128]{2,1,0:T(8,128)(2,1)}, bf16[8,128,128]{2,1,0:T(8,128)(2,1)}, u32[]{:S(2)}, u32[]{:S(2)}) collective-permute-start(bf16[8,128,128]{2,1,0:T(8,128)(2,1)} %get-tuple-element.35), channel_id=1, source_target_pairs={{0,2},{1,3},{2,0},{3,1},{4,6},{5,7},{6,4},{7,5},{8,10},{9,11},{10,... | collective-permute-start | bytes 786440 | tf_op jit(solution)/shard_map/ppermute | solution.py:299
  53.1 63.4 %collective-permute-start.6 = (bf16[4,128,128]{2,1,0:T(8,128)(2,1)}, bf16[4,128,128]{2,1,0:T(8,128)(2,1)S(1)}, u32[]{:S(2)}, u32[]{:S(2)}) collective-permute-start(bf16[4,128,128]{2,1,0:T(8,128)(2,1)} %pad_maximum_fusion.1), channel_id=1, source_target_pairs={{0,4},{1,5},{2,6},{3,7},{4,8},{5,9},{6,10},{7,11},{8,12},{9,13},{1... | collective-permute-start | bytes 393224 | tf_op jit(solution)/shard_map/ppermute | solution.py:299
  58.7 58.5 %collective-permute-start.7 = (bf16[4,128,128]{2,1,0:T(8,128)(2,1)}, bf16[4,128,128]{2,1,0:T(8,128)(2,1)}, u32[]{:S(2)}, u32[]{:S(2)}) collective-permute-start(bf16[4,128,128]{2,1,0:T(8,128)(2,1)} %pad_maximum_fusion.2), channel_id=1, source_target_pairs={{0,8},{1,9},{2,10},{3,11},{4,12},{5,13},{6,14},{7,15},{8,16},{9,17... | collective-permute-start | bytes 393224 | tf_op jit(solution)/shard_map/ppermute | solution.py:299
  63.9 55.6 %collective-permute-start.8 = (bf16[4,128,128]{2,1,0:T(8,128)(2,1)}, bf16[4,128,128]{2,1,0:T(8,128)(2,1)}, u32[]{:S(2)}, u32[]{:S(2)}) collective-permute-start(bf16[4,128,128]{2,1,0:T(8,128)(2,1)} %pad_maximum_fusion.3), channel_id=1, source_target_pairs={{0,12},{1,13},{2,14},{3,15},{4,16},{5,17},{6,18},{7,19},{8,20},{9,... | collective-permute-start | bytes 393224 | tf_op jit(solution)/shard_map/ppermute | solution.py:299
  65.9 53.7 %collective-permute-start.9 = (bf16[4,128,128]{2,1,0:T(8,128)(2,1)}, bf16[4,128,128]{2,1,0:T(8,128)(2,1)}, u32[]{:S(2)}, u32[]{:S(2)}) collective-permute-start(bf16[4,128,128]{2,1,0:T(8,128)(2,1)} %pad_maximum_fusion.4), channel_id=1, source_target_pairs={{0,16},{1,17},{2,18},{3,19},{4,20},{5,21},{6,22},{7,23},{8,24},{9,... | collective-permute-start | bytes 393224 | tf_op jit(solution)/shard_map/ppermute | solution.py:299
  71.7 27.6 %copy-start.4 = (bf16[1,128,128]{2,1,0:T(8,128)(2,1)S(1)}, bf16[1,128,128]{2,1,0:T(8,128)(2,1)}, u32[]{:S(2)}) copy-start(bf16[1,128,128]{2,1,0:T(8,128)(2,1)} %get-tuple-element.43) | copy-start | bytes 98308
  95.9 3.4 %copy-start.5 = (bf16[1,128,128]{2,1,0:T(8,128)(2,1)S(1)}, bf16[1,128,128]{2,1,0:T(8,128)(2,1)}, u32[]{:S(2)}) copy-start(bf16[1,128,128]{2,1,0:T(8,128)(2,1)} %get-tuple-element.59) | copy-start | bytes 98308
  95.9 3.4 %copy-start.6 = (bf16[1,128,128]{2,1,0:T(8,128)(2,1)S(1)}, bf16[1,128,128]{2,1,0:T(8,128)(2,1)}, u32[]{:S(2)}) copy-start(bf16[1,128,128]{2,1,0:T(8,128)(2,1)} %get-tuple-element.51) | copy-start | bytes 98308
  95.9 19.9 %copy-start.3 = (bf16[4,128,128]{2,1,0:T(8,128)(2,1)S(1)}, bf16[4,128,128]{2,1,0:T(8,128)(2,1)}, u32[]{:S(2)}) copy-start(bf16[4,128,128]{2,1,0:T(8,128)(2,1)} %pad_maximum_fusion.5) | copy-start | bytes 393220
  96.4 20.2 %copy-start.2 = (bf16[4,128,128]{2,1,0:T(8,128)(2,1)S(1)}, bf16[4,128,128]{2,1,0:T(8,128)(2,1)}, u32[]{:S(2)}) copy-start(bf16[4,128,128]{2,1,0:T(8,128)(2,1)} %pad_maximum_fusion.6) | copy-start | bytes 393220
  96.4 20.9 %copy-start.1 = (bf16[4,128,128]{2,1,0:T(8,128)(2,1)S(1)}, bf16[4,128,128]{2,1,0:T(8,128)(2,1)}, u32[]{:S(2)}) copy-start(bf16[4,128,128]{2,1,0:T(8,128)(2,1)} %pad_maximum_fusion.7) | copy-start | bytes 393220
  96.4 34.8 %copy-start = (s32[2]{0:T(128)S(1)}, s32[2]{0:T(128)}, u32[]{:S(2)}) copy-start(s32[2]{0:T(128)} %pad_add_fusion.at_ref.refs_0_) | copy-start | bytes 28
  96.4 8.1 %collective-permute-start = (bf16[16,2048]{1,0:T(8,128)(2,1)S(1)}, bf16[16,2048]{1,0:T(8,128)(2,1)S(1)}, u32[]{:S(2)}, u32[]{:S(2)}) collective-permute-start(bf16[16,2048]{1,0:T(8,128)(2,1)S(1)} %get-tuple-element.15), channel_id=1, source_target_pairs={{0,96},{32,0},{64,32},{96,64},{1,97},{33,1},{65,33},{97,65},{2,98}... | collective-permute-start | bytes 196616 | tf_op jit(solution)/shard_map/ppermute | solution.py:289
  104.5 5.8 %collective-permute-start.1 = (bf16[16,2048]{1,0:T(8,128)(2,1)S(1)}, bf16[16,2048]{1,0:T(8,128)(2,1)S(1)}, u32[]{:S(2)}, u32[]{:S(2)}) collective-permute-start(bf16[16,2048]{1,0:T(8,128)(2,1)S(1)} %get-tuple-element.15), channel_id=1, source_target_pairs={{0,64},{32,96},{64,0},{96,32},{1,65},{33,97},{65,1},{97,33},{2,66}... | collective-permute-start | bytes 196616 | tf_op jit(solution)/shard_map/ppermute | solution.py:289
  110.3 5.5 %collective-permute-start.2 = (bf16[16,2048]{1,0:T(8,128)(2,1)S(1)}, bf16[16,2048]{1,0:T(8,128)(2,1)S(1)}, u32[]{:S(2)}, u32[]{:S(2)}) collective-permute-start(bf16[16,2048]{1,0:T(8,128)(2,1)S(1)} %get-tuple-element.15), channel_id=1, source_target_pairs={{0,32},{32,64},{64,96},{96,0},{1,33},{33,65},{65,97},{97,1},{2,34}... | collective-permute-start | bytes 196616 | tf_op jit(solution)/shard_map/ppermute | solution.py:289
  115.8 11.9 %collective-permute-start.10 = (bf16[4,128,128]{2,1,0:T(8,128)(2,1)S(1)}, bf16[4,128,128]{2,1,0:T(8,128)(2,1)S(1)}, u32[]{:S(2)}, u32[]{:S(2)}) collective-permute-start(bf16[4,128,128]{2,1,0:T(8,128)(2,1)S(1)} %copy-done.3), channel_id=1, source_target_pairs={{0,20},{1,21},{2,22},{3,23},{4,24},{5,25},{6,26},{7,27},{8,28},{9,... | collective-permute-start | bytes 393224 | tf_op jit(solution)/shard_map/ppermute | solution.py:299
  116.6 14.6 %collective-permute-start.11 = (bf16[4,128,128]{2,1,0:T(8,128)(2,1)S(1)}, bf16[4,128,128]{2,1,0:T(8,128)(2,1)S(1)}, u32[]{:S(2)}, u32[]{:S(2)}) collective-permute-start(bf16[4,128,128]{2,1,0:T(8,128)(2,1)S(1)} %copy-done.2), channel_id=1, source_target_pairs={{0,24},{1,25},{2,26},{3,27},{4,28},{5,29},{6,30},{7,31},{8,0},{9,1... | collective-permute-start | bytes 393224 | tf_op jit(solution)/shard_map/ppermute | solution.py:299
  117.3 13.9 %collective-permute-start.12 = (bf16[4,128,128]{2,1,0:T(8,128)(2,1)S(1)}, bf16[4,128,128]{2,1,0:T(8,128)(2,1)S(1)}, u32[]{:S(2)}, u32[]{:S(2)}) collective-permute-start(bf16[4,128,128]{2,1,0:T(8,128)(2,1)S(1)} %copy-done.1), channel_id=1, source_target_pairs={{0,28},{1,29},{2,30},{3,31},{4,0},{5,1},{6,2},{7,3},{8,4},{9,5},{1... | collective-permute-start | bytes 393224 | tf_op jit(solution)/shard_map/ppermute | solution.py:299

commit v5 on v4

--- a/solution.py
+++ b/solution.py
@@ -167,7 +167,7 @@
     )(at, w_gate, w_up)
 
 
-def unpack_kernel(extra_ref, factor_ref, scale_ref, router_ref, *, experts):
+def unpack_kernel(extra_ref, factor_ref, gate_scale_ref, up_scale_ref, router_ref, *, experts):
     extra = extra_ref[...].astype(jnp.float32)
     lane = lax.broadcasted_iota(jnp.int32, (32, LANES), 1)
     scale = jnp.zeros((32, LANES), jnp.float32)
@@ -181,7 +181,10 @@
     scale = scale / D_MODEL
     for s in range(32):
         factor_ref[s] = jnp.where(lane < 2 * experts, factor_ref[s] / scale, 0.0)
-    scale_ref[...] = jnp.concatenate([scale] * 4, axis=0).T[: 2 * experts, :32]
+    scale = jnp.take_along_axis(scale, lane % experts * 2 + lane // experts % 2, axis=1)
+    scale = jnp.concatenate([scale] * 4, axis=0).T
+    gate_scale_ref[...] = scale[:experts, :32]
+    up_scale_ref[...] = scale[experts : 2 * experts, :32]
     left = lax.broadcasted_iota(jnp.int32, (8, LANES), 1) < 64
     for p in range(16):
         one, two = extra[2 * p, 16:], extra[2 * p + 1, 16:]
@@ -196,21 +199,26 @@
         name="unpack",
         grid=(1,),
         in_specs=[pl.BlockSpec((32, EXTRA, LANES), lambda _: (0, 32 * (experts - GROUP) // EXTRA, 0))],
-        out_specs=[whole((32, 32, LANES)), whole((2 * experts, 32)), whole((16, D_MODEL))],
+        out_specs=[whole((32, 32, LANES)), whole((experts, 32)), whole((experts, 32)), whole((16, D_MODEL))],
         out_shape=[
             jax.ShapeDtypeStruct((32, 32, LANES), jnp.float32),
-            jax.ShapeDtypeStruct((2 * experts, 32), jnp.float32),
+            jax.ShapeDtypeStruct((experts, 32), jnp.float32),
+            jax.ShapeDtypeStruct((experts, 32), jnp.float32),
             jax.ShapeDtypeStruct((16, D_MODEL), jnp.bfloat16),
         ],
         compiler_params=SOME,
     )(got)
 
 
-def decoded(read, factor_ref, gate_ref, up_ref, value_ref, first):
+def lanes_moved():
     to = lax.broadcasted_iota(jnp.int32, (2 * LANES, 2 * LANES), 1)
     of = lax.broadcasted_iota(jnp.int32, (2 * LANES, 2 * LANES), 0)
     move = of == to % 64 + to // 64 % 2 * LANES + to // LANES * 64
-    move = jnp.where(move, 1.0, 0.0).astype(jnp.bfloat16)
+    return jnp.where(move, 1.0, 0.0).astype(jnp.bfloat16)
+
+
+def decoded(read, factor_ref, gate_ref, up_ref, value_ref, first):
+    move = lanes_moved()
 
     def one(i, _):
         row = pl.multiple_of(i * 32, 32)
@@ -251,18 +259,40 @@
 
 
 def decode_rest_kernel(at_ref, *refs, experts):
-    parts, (factor_ref, _, _, gate_ref, up_ref, got_ref, value_ref) = refs[:DEEP], refs[DEEP:]
+    parts, (factor_ref, _, _, gate_to, up_to, value_ref, gates, ups, out) = refs[:DEEP], refs[DEEP:]
     z, y = at_ref[0], at_ref[1]
-    for k, part in enumerate(parts):
-        for j in range(WIDE):
-            got_ref[(z - k) % DEEP * WIDE + (y - j) % WIDE] = part[j]
-    read = lambda s, row: got_ref[s, pl.ds(row, 32)]
-    decoded(read, factor_ref, gate_ref, up_ref, value_ref, experts - GROUP)
+    move = lanes_moved()
+
+    def leaving(i):
+        return (
+            pltpu.make_async_copy(gates.at[i], gate_to.at[experts - GROUP + i], out.at[0, i]),
+            pltpu.make_async_copy(ups.at[i], up_to.at[experts - GROUP + i], out.at[1, i]),
+        )
+
+    for i in range(GROUP):
+        which = 2 * (experts - GROUP + i) + lax.broadcasted_iota(jnp.int32, (32, LANES), 1) // 64
+        for k, part in enumerate(parts):
+            deep = (z - k) % DEEP
+            for t in range(WIDE):
+                code = part[(y - t) % WIDE, 32 * i : 32 * (i + 1)].astype(jnp.float32)
+                factor = jnp.take_along_axis(factor_ref[deep * WIDE + t], which, axis=1)
+                row = pl.multiple_of((deep * 2 + t // 2) * 32, 32)
+                value = (jnp.log(code) * factor).astype(jnp.bfloat16)
+                value_ref[i, pl.ds(row, 32), t % 2 * LANES : (t % 2 + 1) * LANES] = value
+        both = jnp.dot(value_ref[i], move, preferred_element_type=jnp.float32).astype(jnp.bfloat16)
+        for p in range(16):
+            gates[i, :, p * LANES : (p + 1) * LANES] = both[p * 32 : (p + 1) * 32, :LANES]
+            ups[i, :, p * LANES : (p + 1) * LANES] = both[p * 32 : (p + 1) * 32, LANES:]
+        for copy in leaving(i):
+            copy.start()
+    for i in range(GROUP):
+        for copy in leaving(i):
+            copy.wait()
 
 
 def decode_rest(at, parts, factor, gate, up):
     experts = gate.shape[0]
-    last = experts // GROUP - 1
+    anywhere = pl.BlockSpec(memory_space=pl.ANY)
     return pl.pallas_call(
         lambda *refs: decode_rest_kernel(*refs, experts=experts),
         name="decode_rest",
@@ -270,12 +300,13 @@
             num_scalar_prefetch=1,
             grid=(1,),
             in_specs=[pl.BlockSpec(parts[0].shape, lambda _, at: (0, 0, 0))] * DEEP
-            + [pl.BlockSpec((32, 32, LANES), lambda _, at: (0, 0, 0))]
-            + [pl.BlockSpec(memory_space=pl.ANY)] * 2,
-            out_specs=[pl.BlockSpec((GROUP, 32, D_MODEL), lambda _, at: (last, 0, 0))] * 2,
+            + [pl.BlockSpec((32, 32, LANES), lambda _, at: (0, 0, 0)), anywhere, anywhere],
+            out_specs=[anywhere] * 2,
             scratch_shapes=[
-                pltpu.VMEM((32, 32 * GROUP, LANES), jnp.bfloat16),
                 pltpu.VMEM((GROUP, 512, 2 * LANES), jnp.bfloat16),
+                pltpu.VMEM((GROUP, 32, D_MODEL), jnp.bfloat16),
+                pltpu.VMEM((GROUP, 32, D_MODEL), jnp.bfloat16),
+                pltpu.SemaphoreType.DMA((2, GROUP)),
             ],
         ),
         out_shape=[jax.ShapeDtypeStruct(gate.shape, gate.dtype)] * 2,
@@ -312,12 +343,12 @@
     parts = [jnp.stack([row[k] for row in rows]) for k in range(DEEP)]
     for k in range(1, DEEP):
         parts[k] = offset(parts[k], k, 0)
-    factor, scale, router = unpack(got, experts)
+    factor, scale_gate, scale_up, router = unpack(got, experts)
     gate, up = decode(got, factor, experts)
     router = joined(router, "bank").T
-    at, router, scale = lax.optimization_barrier((at, router, scale.reshape(experts, 2, 32).swapaxes(0, 1)))
+    at, router = lax.optimization_barrier((at, router))
     gate, up = decode_rest(at, parts, factor, gate, up)
-    return jnp.swapaxes(gate, 1, 2), jnp.swapaxes(up, 1, 2), scale[0], scale[1], router
+    return jnp.swapaxes(gate, 1, 2), jnp.swapaxes(up, 1, 2), scale_gate, scale_up, router
 
 
 def solution(mesh):

time: 136 us -> 136 us (level)
  the two profiles are of different devices: /device:TPU:56 before, /device:TPU:72 now
where the time goes in v5:
time: 136 us; the launch traced here: 135 us
  waiting for transfers between devices  62.5 us (46%)
  starting transfers between devices  35 us (26%)
  Pallas kernels  18.9 us (14%)
  other arithmetic  9.11 us (7%)
  local copies, waits for them, and re-layouts  8.84 us (6%)
    ppermute x10, waiting for transfers between devices, offset(): return lax.ppermute(array, 'zero', pairs)  29.1 us
    all_to_all x1, waiting for transfers between devices, local(): got = lax.all_to_all(sent, 'zero', 0, 0, tiled=True)  22.9 us
    ppermute x10, starting transfers between devices, offset(): return lax.ppermute(array, 'zero', pairs)  20.5 us
    all_to_all x1, starting transfers between devices, local(): got = lax.all_to_all(sent, 'zero', 0, 0, tiled=True)  10.8 us
    ppermute x3, waiting for transfers between devices, joined(): lax.ppermute(array, axis, [(s, (s + k) % count) for s in range(count)])  10.5 us
    another operation x8, other arithmetic, local(): parts = [jnp.stack([row[k] for row in rows]) for k in range(DEEP)]  8.48 us
    slice x4, local copies, waits for them, and re-layouts, local(): parts = [jnp.stack([row[k] for row in rows]) for k in range(DEEP)]  6.05 us
    pallas_call x1, Pallas kernels, encode(): pl.pallas_call(lambda *refs: encode_kernel(*refs, bands=columns // LANES)...  5.31 us
  transfers between devices with their start and end apart: 14, of which 8 were waited for; matrix products, arithmetic and copies ran while one was open for 13% of the time, Pallas kernels for 8%

profile of v5, /device:TPU:72, one launch (start us, length us, event | category | flops | bytes accessed | tf_op | source)
XLA Modules:
  0.0 135.2 jit_solution(499521300010708550)
XLA Ops:
  0.6 5.3 %encode.1 = bf16[32,408,128]{2,1,0:T(8,128)(2,1)} custom-call(f32[16,64,1024]{2,1,0:T(8,128)} %gate_ref.1, f32[16,64,1024]{2,1,0:T(8,128)} %up_ref.1, f32[16,64]{1,0:T(8,128)} %bitcast.10, f32[1,64]{1,0:T(1,128)} %bitcast.11), custom_call_target="tpu_custom_call" | custom-call | tf_op jit(solution)/shard_map/encode/pallas_call | solution.py:120
  5.9 10.8 %all-to-all-start = ((bf16[32,408,128]{2,1,0:T(8,128)(2,1)}), bf16[32,408,128]{2,1,0:T(8,128)(2,1)S(1)}, u32[]{:S(2)}, u32[]{:S(2)}) async-start(bf16[32,408,128]{2,1,0:T(8,128)(2,1)} %encode.1), calls=%async_computation | async-start | bytes 6684672 | tf_op jit(solution)/shard_map/all_to_all | solution.py:338
  17.4 3.9 %encode_rest.1 = bf16[32,128,128]{2,1,0:T(8,128)(2,1)} custom-call(s32[2]{0:T(128)} %pad_add_fusion.at_ref.refs_0_, f32[16,64,1024]{2,1,0:T(8,128)} %gate_ref.1, f32[16,64,1024]{2,1,0:T(8,128)} %up_ref.1), custom_call_target="tpu_custom_call" | custom-call | tf_op jit(solution)/shard_map/encode_rest/pallas_call | solution.py:155
  21.3 2.0 %fusion.1 = (bf16[8,128,128]{2,1,0:T(8,128)(2,1)}, bf16[8,128,128]{2,1,0:T(8,128)(2,1)}, bf16[8,128,128]{2,1,0:T(8,128)(2,1)}) fusion(bf16[32,128,128]{2,1,0:T(8,128)(2,1)} %encode_rest.1), kind=kLoop, calls=%fused_computation.18 | loop fusion | bytes 1572864 | tf_op jit(solution)/shard_map/slice | solution.py:342
  23.3 1.5 %collective-permute-start.3 = (bf16[8,128,128]{2,1,0:T(8,128)(2,1)}, bf16[8,128,128]{2,1,0:T(8,128)(2,1)}, u32[]{:S(2)}, u32[]{:S(2)}) collective-permute-start(bf16[8,128,128]{2,1,0:T(8,128)(2,1)} %get-tuple-element.33), channel_id=1, source_target_pairs={{0,1},{1,2},{2,3},{3,0},{4,5},{5,6},{6,7},{7,4},{8,9},{9,10},{10,1... | collective-permute-start | bytes 786440 | tf_op jit(solution)/shard_map/ppermute | solution.py:330
  25.3 2.1 %collective-permute-start.4 = (bf16[8,128,128]{2,1,0:T(8,128)(2,1)}, bf16[8,128,128]{2,1,0:T(8,128)(2,1)}, u32[]{:S(2)}, u32[]{:S(2)}) collective-permute-start(bf16[8,128,128]{2,1,0:T(8,128)(2,1)} %get-tuple-element.35), channel_id=1, source_target_pairs={{0,2},{1,3},{2,0},{3,1},{4,6},{5,7},{6,4},{7,5},{8,10},{9,11},{10,... | collective-permute-start | bytes 786440 | tf_op jit(solution)/shard_map/ppermute | solution.py:330
  27.4 1.5 %fusion = (bf16[1,128,128]{2,1,0:T(8,128)(2,1)}, bf16[1,128,128]{2,1,0:T(8,128)(2,1)}, bf16[1,128,128]{2,1,0:T(8,128)(2,1)S(1)}, bf16[1,128,128]{2,1,0:T(8,128)(...) fusion(bf16[32,128,128]{2,1,0:T(8,128)(2,1)} %encode_rest.1), kind=kLoop, calls=%fused_computation.17 | loop fusion | bytes 524288 | tf_op jit(solution)/shard_map/slice | solution.py:343
  29.0 9.3 %collective-permute-done.3 = bf16[8,128,128]{2,1,0:T(8,128)(2,1)} collective-permute-done((bf16[8,128,128]{2,1,0:T(8,128)(2,1)}, bf16[8,128,128]{2,1,0:T(8,128)(2,1)}, u32[]{:S(2)}, u32[]{:S(2)}) %collective-permute-start.3) | collective-permute-done | bytes 262176 | tf_op jit(solution)/shard_map/ppermute | solution.py:330
  38.3 1.5 %fusion.2 = (bf16[1,128,128]{2,1,0:T(8,128)(2,1)S(1)}, bf16[1,128,128]{2,1,0:T(8,128)(2,1)S(1)}, bf16[1,128,128]{2,1,0:T(8,128)(2,1)S(1)}, bf16[1,128,128]{2,1,0...) fusion(bf16[8,128,128]{2,1,0:T(8,128)(2,1)} %collective-permute, ...), kind=kLoop, calls=%fused_computation.19 | loop fusion | bytes 524288 | tf_op jit(solution)/shard_map/slice | solution.py:343
  39.8 1.5 %fusion.4 = (bf16[1,128,128]{2,1,0:T(8,128)(2,1)S(1)}, bf16[1,128,128]{2,1,0:T(8,128)(2,1)S(1)}, bf16[1,128,128]{2,1,0:T(8,128)(2,1)S(1)}, bf16[1,128,128]{2,1,0...) fusion(bf16[8,128,128]{2,1,0:T(8,128)(2,1)} %collective-permute, ...), kind=kLoop, calls=%fused_computation.21 | loop fusion | bytes 524288 | tf_op jit(solution)/shard_map/slice | solution.py:343
  41.3 8.3 %collective-permute-done.4 = bf16[8,128,128]{2,1,0:T(8,128)(2,1)} collective-permute-done((bf16[8,128,128]{2,1,0:T(8,128)(2,1)}, bf16[8,128,128]{2,1,0:T(8,128)(2,1)}, u32[]{:S(2)}, u32[]{:S(2)}) %collective-permute-start.4) | collective-permute-done | bytes 262176 | tf_op jit(solution)/shard_map/ppermute | solution.py:330
  49.6 1.5 %fusion.3 = (bf16[1,128,128]{2,1,0:T(8,128)(2,1)S(1)}, bf16[1,128,128]{2,1,0:T(8,128)(2,1)S(1)}, bf16[1,128,128]{2,1,0:T(8,128)(2,1)S(1)}, bf16[1,128,128]{2,1,0...) fusion(bf16[8,128,128]{2,1,0:T(8,128)(2,1)} %collective-permute, ...), kind=kLoop, calls=%fused_computation.20 | loop fusion | bytes 524288 | tf_op jit(solution)/shard_map/slice | solution.py:343
  52.4 1.4 %pad_maximum_fusion.2 = bf16[4,128,128]{2,1,0:T(8,128)(2,1)} fusion(bf16[1,128,128]{2,1,0:T(8,128)(2,1)S(1)} %get-tuple-element.57, bf16[1,128,128]{2,1,0:T(8,128)(2,1)S(1)} %get-tuple-element.49, bf16[1,128,128]{2,1,0:T(8,128)(2,1)S(1)} %get-tuple-element.41, bf16[1,128,128]{2,1,0:T(8,128)(2,1)} %get-tuple-element.30), kind=kLoop, calls=%fused_computation.3 | loop fusion | flops 196608 | bytes 262144 | tf_op jit(solution)/shard_map/stack | solution.py:343
  53.8 3.3 %collective-permute-start.7 = (bf16[4,128,128]{2,1,0:T(8,128)(2,1)}, bf16[4,128,128]{2,1,0:T(8,128)(2,1)}, u32[]{:S(2)}, u32[]{:S(2)}) collective-permute-start(bf16[4,128,128]{2,1,0:T(8,128)(2,1)} %pad_maximum_fusion.2), channel_id=1, source_target_pairs={{0,8},{1,9},{2,10},{3,11},{4,12},{5,13},{6,14},{7,15},{8,16},{9,17... | collective-permute-start | bytes 393224 | tf_op jit(solution)/shard_map/ppermute | solution.py:330
  57.1 1.4 %pad_maximum_fusion.3 = bf16[4,128,128]{2,1,0:T(8,128)(2,1)} fusion(bf16[1,128,128]{2,1,0:T(8,128)(2,1)S(1)} %get-tuple-element.56, bf16[1,128,128]{2,1,0:T(8,128)(2,1)S(1)} %get-tuple-element.48, bf16[1,128,128]{2,1,0:T(8,128)(2,1)S(1)} %get-tuple-element.40, bf16[1,128,128]{2,1,0:T(8,128)(2,1)} %get-tuple-element.29), kind=kLoop, calls=%fused_computation.4 | loop fusion | flops 196608 | bytes 262144 | tf_op jit(solution)/shard_map/stack | solution.py:343
  58.5 0.9 collective-permute-start.8
  59.4 1.4 %pad_maximum_fusion.4 = bf16[4,128,128]{2,1,0:T(8,128)(2,1)} fusion(bf16[1,128,128]{2,1,0:T(8,128)(2,1)S(1)} %get-tuple-element.55, bf16[1,128,128]{2,1,0:T(8,128)(2,1)S(1)} %get-tuple-element.47, bf16[1,128,128]{2,1,0:T(8,128)(2,1)S(1)} %get-tuple-element.39, bf16[1,128,128]{2,1,0:T(8,128)(2,1)} %get-tuple-element.28), kind=kLoop, calls=%fused_computation.5 | loop fusion | flops 196608 | bytes 262144 | tf_op jit(solution)/shard_map/stack | solution.py:343
  60.8 5.6 %collective-permute-start.9 = (bf16[4,128,128]{2,1,0:T(8,128)(2,1)}, bf16[4,128,128]{2,1,0:T(8,128)(2,1)}, u32[]{:S(2)}, u32[]{:S(2)}) collective-permute-start(bf16[4,128,128]{2,1,0:T(8,128)(2,1)} %pad_maximum_fusion.4), channel_id=1, source_target_pairs={{0,16},{1,17},{2,18},{3,19},{4,20},{5,21},{6,22},{7,23},{8,24},{9,... | collective-permute-start | bytes 393224 | tf_op jit(solution)/shard_map/ppermute | solution.py:330
  66.4 1.4 %pad_maximum_fusion.7 = bf16[4,128,128]{2,1,0:T(8,128)(2,1)} fusion(bf16[1,128,128]{2,1,0:T(8,128)(2,1)S(1)} %get-tuple-element.52, bf16[1,128,128]{2,1,0:T(8,128)(2,1)S(1)} %get-tuple-element.44, bf16[1,128,128]{2,1,0:T(8,128)(2,1)S(1)} %get-tuple-element.36, bf16[1,128,128]{2,1,0:T(8,128)(2,1)} %get-tuple-element.25), kind=kLoop, calls=%fused_computation.8 | loop fusion | flops 196608 | bytes 262144 | tf_op jit(solution)/shard_map/stack | solution.py:343
  67.9 1.4 %pad_maximum_fusion.6 = bf16[4,128,128]{2,1,0:T(8,128)(2,1)} fusion(bf16[1,128,128]{2,1,0:T(8,128)(2,1)S(1)} %get-tuple-element.53, bf16[1,128,128]{2,1,0:T(8,128)(2,1)S(1)} %get-tuple-element.45, bf16[1,128,128]{2,1,0:T(8,128)(2,1)S(1)} %get-tuple-element.37, bf16[1,128,128]{2,1,0:T(8,128)(2,1)} %get-tuple-element.26), kind=kLoop, calls=%fused_computation.7 | loop fusion | flops 196608 | bytes 262144 | tf_op jit(solution)/shard_map/stack | solution.py:343
  70.0 22.9 %all-to-all-done.refs_0_ = bf16[32,408,128]{2,1,0:T(8,128)(2,1)S(1)} async-done(((bf16[32,408,128]{2,1,0:T(8,128)(2,1)}), bf16[32,408,128]{2,1,0:T(8,128)(2,1)S(1)}, u32[]{:S(2)}, u32[]{:S(2)}) %all-to-all-start) | async-done | bytes 3342368 | tf_op jit(solution)/shard_map/all_to_all | solution.py:338
  92.9 1.2 unpack.1
  94.1 2.8 %collective-permute-start = (bf16[16,2048]{1,0:T(8,128)(2,1)S(1)}, bf16[16,2048]{1,0:T(8,128)(2,1)S(1)}, u32[]{:S(2)}, u32[]{:S(2)}) collective-permute-start(bf16[16,2048]{1,0:T(8,128)(2,1)S(1)} %get-tuple-element.15), channel_id=1, source_target_pairs={{0,96},{32,0},{64,32},{96,64},{1,97},{33,1},{65,33},{97,65},{2,98}... | collective-permute-start | bytes 196616 | tf_op jit(solution)/shard_map/ppermute | solution.py:320
  96.9 5.2 %decode.1 = (bf16[16,32,2048]{2,1,0:T(8,128)(2,1)}, bf16[16,32,2048]{2,1,0:T(8,128)(2,1)}) custom-call(bf16[32,408,128]{2,1,0:T(8,128)(2,1)S(1)} %all-to-all-done.refs_0_, f32[32,32,128]{2,1,0:T(8,128)S(1)} %get-tuple-element.17.refs_1_.refs_9_), custom_call_target="tpu_custom_call" | custom-call | tf_op jit(solution)/shard_map/decode/pallas_call | solution.py:246
  103.0 5.0 %collective-permute-done.1 = bf16[16,2048]{1,0:T(8,128)(2,1)S(1)} collective-permute-done((bf16[16,2048]{1,0:T(8,128)(2,1)S(1)}, bf16[16,2048]{1,0:T(8,128)(2,1)S(1)}, u32[]{:S(2)}, u32[]{:S(2)}) %collective-permute-start.1) | collective-permute-done | bytes 65568 | tf_op jit(solution)/shard_map/ppermute | solution.py:320
  108.0 5.5 %collective-permute-done.2 = bf16[16,2048]{1,0:T(8,128)(2,1)S(1)} collective-permute-done((bf16[16,2048]{1,0:T(8,128)(2,1)S(1)}, bf16[16,2048]{1,0:T(8,128)(2,1)S(1)}, u32[]{:S(2)}, u32[]{:S(2)}) %collective-permute-start.2) | collective-permute-done | bytes 65568 | tf_op jit(solution)/shard_map/ppermute | solution.py:320
  113.5 1.8 %collective-permute-start.10 = (bf16[4,128,128]{2,1,0:T(8,128)(2,1)S(1)}, bf16[4,128,128]{2,1,0:T(8,128)(2,1)S(1)}, u32[]{:S(2)}, u32[]{:S(2)}) collective-permute-start(bf16[4,128,128]{2,1,0:T(8,128)(2,1)S(1)} %copy-done.3), channel_id=1, source_target_pairs={{0,20},{1,21},{2,22},{3,23},{4,24},{5,25},{6,26},{7,27},{8,28},{9,... | collective-permute-start | bytes 393224 | tf_op jit(solution)/shard_map/ppermute | solution.py:330
  115.3 4.3 %collective-permute-start.11 = (bf16[4,128,128]{2,1,0:T(8,128)(2,1)S(1)}, bf16[4,128,128]{2,1,0:T(8,128)(2,1)S(1)}, u32[]{:S(2)}, u32[]{:S(2)}) collective-permute-start(bf16[4,128,128]{2,1,0:T(8,128)(2,1)S(1)} %copy-done.2), channel_id=1, source_target_pairs={{0,24},{1,25},{2,26},{3,27},{4,28},{5,29},{6,30},{7,31},{8,0},{9,1... | collective-permute-start | bytes 393224 | tf_op jit(solution)/shard_map/ppermute | solution.py:330
  120.3 4.5 %collective-permute-done.10.refs_6_ = bf16[4,128,128]{2,1,0:T(8,128)(2,1)S(1)} collective-permute-done((bf16[4,128,128]{2,1,0:T(8,128)(2,1)S(1)}, bf16[4,128,128]{2,1,0:T(8,128)(2,1)S(1)}, u32[]{:S(2)}, u32[]{:S(2)}) %collective-permute-start.10) | collective-permute-done | bytes 131104 | tf_op jit(solution)/shard_map/ppermute | solution.py:330
  124.8 4.6 %collective-permute-done.11.refs_7_ = bf16[4,128,128]{2,1,0:T(8,128)(2,1)S(1)} collective-permute-done((bf16[4,128,128]{2,1,0:T(8,128)(2,1)S(1)}, bf16[4,128,128]{2,1,0:T(8,128)(2,1)S(1)}, u32[]{:S(2)}, u32[]{:S(2)}) %collective-permute-start.11) | collective-permute-done | bytes 131104 | tf_op jit(solution)/shard_map/ppermute | solution.py:330
  129.4 2.3 %collective-permute-done.12.refs_8_ = bf16[4,128,128]{2,1,0:T(8,128)(2,1)S(1)} collective-permute-done((bf16[4,128,128]{2,1,0:T(8,128)(2,1)S(1)}, bf16[4,128,128]{2,1,0:T(8,128)(2,1)S(1)}, u32[]{:S(2)}, u32[]{:S(2)}) %collective-permute-start.12) | collective-permute-done | bytes 131104 | tf_op jit(solution)/shard_map/ppermute | solution.py:330
  131.7 3.3 %decode_rest.1 = (bf16[16,32,2048]{2,1,0:T(8,128)(2,1)}, bf16[16,32,2048]{2,1,0:T(8,128)(2,1)}) custom-call(s32[2]{0:T(128)S(1)} %copy-done, bf16[4,128,128]{2,1,0:T(8,128)(2,1)S(1)} %pad_maximum_fusion.refs_1_, bf16[4,128,128]{2,1,0:T(8,128)(2,1)S(1)} %collective-permute-done.6.refs_2_, ...), custom_call_target="tpu_custom_call", output_to_operand_aliasing={{0}: (10, {}), {1}: (11, {})} | custom-call | tf_op jit(solution)/shard_map/decode_rest/pallas_call | solution.py:296
  (37 shorter events, 4.8 us)
Async XLA Ops:
  5.9 86.9 %all-to-all-start = ((bf16[32,408,128]{2,1,0:T(8,128)(2,1)}), bf16[32,408,128]{2,1,0:T(8,128)(2,1)S(1)}, u32[]{:S(2)}, u32[]{:S(2)}) async-start(bf16[32,408,128]{2,1,0:T(8,128)(2,1)} %encode.1), calls=%async_computation | async-start | bytes 6684672 | tf_op jit(solution)/shard_map/all_to_all | solution.py:338
  23.3 15.0 %collective-permute-start.3 = (bf16[8,128,128]{2,1,0:T(8,128)(2,1)}, bf16[8,128,128]{2,1,0:T(8,128)(2,1)}, u32[]{:S(2)}, u32[]{:S(2)}) collective-permute-start(bf16[8,128,128]{2,1,0:T(8,128)(2,1)} %get-tuple-element.33), channel_id=1, source_target_pairs={{0,1},{1,2},{2,3},{3,0},{4,5},{5,6},{6,7},{7,4},{8,9},{9,10},{10,1... | collective-permute-start | bytes 786440 | tf_op jit(solution)/shard_map/ppermute | solution.py:330
  24.8 15.0 %collective-permute-start.5 = (bf16[8,128,128]{2,1,0:T(8,128)(2,1)}, bf16[8,128,128]{2,1,0:T(8,128)(2,1)}, u32[]{:S(2)}, u32[]{:S(2)}) collective-permute-start(bf16[8,128,128]{2,1,0:T(8,128)(2,1)} %get-tuple-element.34), channel_id=1, source_target_pairs={{0,3},{1,0},{2,1},{3,2},{4,7},{5,4},{6,5},{7,6},{8,11},{9,8},{10,9... | collective-permute-start | bytes 786440 | tf_op jit(solution)/shard_map/ppermute | solution.py:330
  25.3 24.3 %collective-permute-start.4 = (bf16[8,128,128]{2,1,0:T(8,128)(2,1)}, bf16[8,128,128]{2,1,0:T(8,128)(2,1)}, u32[]{:S(2)}, u32[]{:S(2)}) collective-permute-start(bf16[8,128,128]{2,1,0:T(8,128)(2,1)} %get-tuple-element.35), channel_id=1, source_target_pairs={{0,2},{1,3},{2,0},{3,1},{4,6},{5,7},{6,4},{7,5},{8,10},{9,11},{10,... | collective-permute-start | bytes 786440 | tf_op jit(solution)/shard_map/ppermute | solution.py:330
  51.8 63.5 %collective-permute-start.6 = (bf16[4,128,128]{2,1,0:T(8,128)(2,1)}, bf16[4,128,128]{2,1,0:T(8,128)(2,1)S(1)}, u32[]{:S(2)}, u32[]{:S(2)}) collective-permute-start(bf16[4,128,128]{2,1,0:T(8,128)(2,1)} %pad_maximum_fusion.1), channel_id=1, source_target_pairs={{0,4},{1,5},{2,6},{3,7},{4,8},{5,9},{6,10},{7,11},{8,12},{9,13},{1... | collective-permute-start | bytes 393224 | tf_op jit(solution)/shard_map/ppermute | solution.py:330
  53.8 65.8 %collective-permute-start.7 = (bf16[4,128,128]{2,1,0:T(8,128)(2,1)}, bf16[4,128,128]{2,1,0:T(8,128)(2,1)}, u32[]{:S(2)}, u32[]{:S(2)}) collective-permute-start(bf16[4,128,128]{2,1,0:T(8,128)(2,1)} %pad_maximum_fusion.2), channel_id=1, source_target_pairs={{0,8},{1,9},{2,10},{3,11},{4,12},{5,13},{6,14},{7,15},{8,16},{9,17... | collective-permute-start | bytes 393224 | tf_op jit(solution)/shard_map/ppermute | solution.py:330
  58.5 61.8 %collective-permute-start.8 = (bf16[4,128,128]{2,1,0:T(8,128)(2,1)}, bf16[4,128,128]{2,1,0:T(8,128)(2,1)}, u32[]{:S(2)}, u32[]{:S(2)}) collective-permute-start(bf16[4,128,128]{2,1,0:T(8,128)(2,1)} %pad_maximum_fusion.3), channel_id=1, source_target_pairs={{0,12},{1,13},{2,14},{3,15},{4,16},{5,17},{6,18},{7,19},{8,20},{9,... | collective-permute-start | bytes 393224 | tf_op jit(solution)/shard_map/ppermute | solution.py:330
  60.8 59.5 %collective-permute-start.9 = (bf16[4,128,128]{2,1,0:T(8,128)(2,1)}, bf16[4,128,128]{2,1,0:T(8,128)(2,1)}, u32[]{:S(2)}, u32[]{:S(2)}) collective-permute-start(bf16[4,128,128]{2,1,0:T(8,128)(2,1)} %pad_maximum_fusion.4), channel_id=1, source_target_pairs={{0,16},{1,17},{2,18},{3,19},{4,20},{5,21},{6,22},{7,23},{8,24},{9,... | collective-permute-start | bytes 393224 | tf_op jit(solution)/shard_map/ppermute | solution.py:330
  70.0 27.0 %copy-start.4 = (bf16[1,128,128]{2,1,0:T(8,128)(2,1)S(1)}, bf16[1,128,128]{2,1,0:T(8,128)(2,1)}, u32[]{:S(2)}) copy-start(bf16[1,128,128]{2,1,0:T(8,128)(2,1)} %get-tuple-element.43) | copy-start | bytes 98308
  92.9 4.0 %copy-start.5 = (bf16[1,128,128]{2,1,0:T(8,128)(2,1)S(1)}, bf16[1,128,128]{2,1,0:T(8,128)(2,1)}, u32[]{:S(2)}) copy-start(bf16[1,128,128]{2,1,0:T(8,128)(2,1)} %get-tuple-element.59) | copy-start | bytes 98308
  92.9 4.0 %copy-start.6 = (bf16[1,128,128]{2,1,0:T(8,128)(2,1)S(1)}, bf16[1,128,128]{2,1,0:T(8,128)(2,1)}, u32[]{:S(2)}) copy-start(bf16[1,128,128]{2,1,0:T(8,128)(2,1)} %get-tuple-element.51) | copy-start | bytes 98308
  92.9 20.6 %copy-start.3 = (bf16[4,128,128]{2,1,0:T(8,128)(2,1)S(1)}, bf16[4,128,128]{2,1,0:T(8,128)(2,1)}, u32[]{:S(2)}) copy-start(bf16[4,128,128]{2,1,0:T(8,128)(2,1)} %pad_maximum_fusion.5) | copy-start | bytes 393220
  94.1 21.2 %copy-start.2 = (bf16[4,128,128]{2,1,0:T(8,128)(2,1)S(1)}, bf16[4,128,128]{2,1,0:T(8,128)(2,1)}, u32[]{:S(2)}) copy-start(bf16[4,128,128]{2,1,0:T(8,128)(2,1)} %pad_maximum_fusion.6) | copy-start | bytes 393220
  94.1 25.5 %copy-start.1 = (bf16[4,128,128]{2,1,0:T(8,128)(2,1)S(1)}, bf16[4,128,128]{2,1,0:T(8,128)(2,1)}, u32[]{:S(2)}) copy-start(bf16[4,128,128]{2,1,0:T(8,128)(2,1)} %pad_maximum_fusion.7) | copy-start | bytes 393220
  94.1 37.7 %copy-start = (s32[2]{0:T(128)S(1)}, s32[2]{0:T(128)}, u32[]{:S(2)}) copy-start(s32[2]{0:T(128)} %pad_add_fusion.at_ref.refs_0_) | copy-start | bytes 28
  94.1 8.1 %collective-permute-start = (bf16[16,2048]{1,0:T(8,128)(2,1)S(1)}, bf16[16,2048]{1,0:T(8,128)(2,1)S(1)}, u32[]{:S(2)}, u32[]{:S(2)}) collective-permute-start(bf16[16,2048]{1,0:T(8,128)(2,1)S(1)} %get-tuple-element.15), channel_id=1, source_target_pairs={{0,96},{32,0},{64,32},{96,64},{1,97},{33,1},{65,33},{97,65},{2,98}... | collective-permute-start | bytes 196616 | tf_op jit(solution)/shard_map/ppermute | solution.py:320
  102.2 5.8 %collective-permute-start.1 = (bf16[16,2048]{1,0:T(8,128)(2,1)S(1)}, bf16[16,2048]{1,0:T(8,128)(2,1)S(1)}, u32[]{:S(2)}, u32[]{:S(2)}) collective-permute-start(bf16[16,2048]{1,0:T(8,128)(2,1)S(1)} %get-tuple-element.15), channel_id=1, source_target_pairs={{0,64},{32,96},{64,0},{96,32},{1,65},{33,97},{65,1},{97,33},{2,66}... | collective-permute-start | bytes 196616 | tf_op jit(solution)/shard_map/ppermute | solution.py:320
  108.0 5.5 %collective-permute-start.2 = (bf16[16,2048]{1,0:T(8,128)(2,1)S(1)}, bf16[16,2048]{1,0:T(8,128)(2,1)S(1)}, u32[]{:S(2)}, u32[]{:S(2)}) collective-permute-start(bf16[16,2048]{1,0:T(8,128)(2,1)S(1)} %get-tuple-element.15), channel_id=1, source_target_pairs={{0,32},{32,64},{64,96},{96,0},{1,33},{33,65},{65,97},{97,1},{2,34}... | collective-permute-start | bytes 196616 | tf_op jit(solution)/shard_map/ppermute | solution.py:320
  113.5 11.4 %collective-permute-start.10 = (bf16[4,128,128]{2,1,0:T(8,128)(2,1)S(1)}, bf16[4,128,128]{2,1,0:T(8,128)(2,1)S(1)}, u32[]{:S(2)}, u32[]{:S(2)}) collective-permute-start(bf16[4,128,128]{2,1,0:T(8,128)(2,1)S(1)} %copy-done.3), channel_id=1, source_target_pairs={{0,20},{1,21},{2,22},{3,23},{4,24},{5,25},{6,26},{7,27},{8,28},{9,... | collective-permute-start | bytes 393224 | tf_op jit(solution)/shard_map/ppermute | solution.py:330
  115.3 14.1 %collective-permute-start.11 = (bf16[4,128,128]{2,1,0:T(8,128)(2,1)S(1)}, bf16[4,128,128]{2,1,0:T(8,128)(2,1)S(1)}, u32[]{:S(2)}, u32[]{:S(2)}) collective-permute-start(bf16[4,128,128]{2,1,0:T(8,128)(2,1)S(1)} %copy-done.2), channel_id=1, source_target_pairs={{0,24},{1,25},{2,26},{3,27},{4,28},{5,29},{6,30},{7,31},{8,0},{9,1... | collective-permute-start | bytes 393224 | tf_op jit(solution)/shard_map/ppermute | solution.py:330
  119.6 12.1 %collective-permute-start.12 = (bf16[4,128,128]{2,1,0:T(8,128)(2,1)S(1)}, bf16[4,128,128]{2,1,0:T(8,128)(2,1)S(1)}, u32[]{:S(2)}, u32[]{:S(2)}) collective-permute-start(bf16[4,128,128]{2,1,0:T(8,128)(2,1)S(1)} %copy-done.1), channel_id=1, source_target_pairs={{0,28},{1,29},{2,30},{3,31},{4,0},{5,1},{6,2},{7,3},{8,4},{9,5},{1... | collective-permute-start | bytes 393224 | tf_op jit(solution)/shard_map/ppermute | solution.py:330
